TPU v7x, 128 devices: a whole 4x4x4 slice. The times are simulated.
128 devices in a mesh: lat: 8 (over y, core), lon: 16 (over z, x).
Axes of the slice: x: 4, y: 4, z: 4, core: 2. Of those that a mesh axis runs over, the one named last changes fastest.
Arguments:
- coarse: bfloat16 [122880, 1104], P(('lat', 'lon')), may hold values from -6 to 6
- w_mix: bfloat16 [69, 64], replicated, may hold values from -0.75 to 0.75
- interp: bfloat16 [16, 256], replicated, may hold values from -1.5 to 1.5
- kernel: bfloat16 [3, 3, 64, 64], replicated, may hold values from -0.25 to 0.25
- bias: float32 [64], replicated, may hold values from -3 to 3
- block_ids: int32 [128, 144], replicated, may hold values from 0 to 122879, as said below
- valid: int32 [128, 144], replicated, may hold values from 0 to 1, as said below
Outputs:
- fine_out: bfloat16 [64, 2304, 2048], P(None, 'lat', 'lon')
Inputs may be any that keep to these rules, and one draw needn't show every extreme that they name: `block_ids`: the coarse grid has 192 block rows and 640 block columns, held block-cyclically: block (r, c) is row ((r mod 8) * 16 + c mod 16) * 960 + (r div 8) * 40 + c div 16 of coarse. Slot p of tile t holds block (r0 + (t div 16) * 18 + p div 8, (c0 + (t mod 16) * 8 + p mod 8) mod (640)), with offsets r0 and c0 common to all tiles. Among the valid slots of one tile at most 3 name blocks of one device, and in every tile exactly 3 valid slots name blocks of some one device. Every tile has 3 or more valid slots.
All inputs are finite; a program needn't handle non-finite values.
Results may differ from a plain program's by a relative error of at most 0.0055.
Values may be sent and summed in bfloat16 or wider, within the bound.
No kernel may reach another device: no remote copies, remote signals or barrier semaphores. Data moves between devices by JAX's collectives and lax.ppermute only.
A program may use at most 192 MiB of HBM per device.

v0:
```python
import jax
import jax.numpy as jnp
from jax import lax
from jax.sharding import PartitionSpec as P

PR = 18
PC = 8


def with_halo(block, sides, width):
    for axis, dim in sides:
        count = lax.axis_size(axis)
        forward = [(i, i + 1) for i in range(count - 1)]
        backward = [(target, source) for source, target in forward]
        low = lax.ppermute(
            lax.slice_in_dim(block, block.shape[dim] - width, None, axis=dim), axis, forward
        )
        high = lax.ppermute(lax.slice_in_dim(block, 0, width, axis=dim), axis, backward)
        block = jnp.concatenate([low, block, high], axis=dim)
    return block


def mix_rows(rows, w_mix):
    count = rows.shape[0]
    flat = rows.reshape(count * 16, w_mix.shape[0])
    mapped = jnp.dot(flat, w_mix, preferred_element_type=jnp.float32).astype(jnp.bfloat16)
    return mapped.reshape(count, 16 * w_mix.shape[1])


def slot_rank(owner, live):
    count = owner.shape[1]
    same = (owner[:, :, None] == owner[:, None, :]) & live[:, None, :]
    earlier = jnp.arange(count)[None, :] < jnp.arange(count)[:, None]
    return jnp.sum(same & earlier[None], axis=2)


def per_device(coarse, w_mix, interp, kernel, bias, block_ids, valid):
    n_lat = lax.axis_size("lat")
    n_lon = lax.axis_size("lon")
    n_dev = n_lat * n_lon
    most = (PR + n_lat - 1) // n_lat * ((PC + n_lon - 1) // n_lon)
    myself = lax.axis_index(("lat", "lon"))
    held = coarse.shape[0]
    channels = w_mix.shape[1]
    owner = block_ids // held
    local = block_ids % held
    live = valid > 0
    rank = slot_rank(owner, live)
    mine = live & (owner == myself)
    places = jnp.arange(most, dtype=jnp.int32)
    hits = mine[:, None, :] & (rank[:, None, :] == places[None, :, None])
    found = jnp.sum(jnp.where(hits, local[:, None, :], 0), axis=2)
    table = jnp.where(jnp.any(hits, axis=2), found, held)
    stacked = jnp.concatenate([coarse, jnp.zeros((1, coarse.shape[1]), coarse.dtype)], axis=0)
    outgoing = stacked[table]
    incoming = lax.all_to_all(outgoing, ("lat", "lon"), split_axis=0, concat_axis=0, tiled=True)
    incoming = incoming.reshape(n_dev * most, coarse.shape[1])
    arrived = mix_rows(incoming, w_mix)
    own_owner = lax.dynamic_index_in_dim(owner, myself, 0, False)
    own_rank = lax.dynamic_index_in_dim(rank, myself, 0, False)
    own_live = lax.dynamic_index_in_dim(valid, myself, 0, False)
    where_from = jnp.where(own_live > 0, own_owner * most + own_rank, 0)
    picked = arrived[where_from].reshape(PR * PC, 16, channels)
    picked = picked * own_live[:, None, None].astype(jnp.bfloat16)
    height = 16 * PR
    breadth = 16 * PC
    left = (
        picked.reshape(PR, PC, 16, channels).transpose(3, 0, 1, 2).reshape(channels * PR, breadth)
    )
    same_col = (jnp.arange(PC)[:, None] == jnp.arange(PC)[None, :]).astype(jnp.bfloat16)
    cells = interp.reshape(16, 16, 16)
    spread = same_col[:, None, None, :, None] * cells[None, :, :, None, :]
    spread = spread.reshape(breadth, 16 * breadth)
    image = jnp.dot(left, spread, preferred_element_type=jnp.float32).astype(jnp.bfloat16)
    image = image.reshape(channels, height, breadth)
    padded = with_halo(image, (("lat", 1), ("lon", 2)), 1)
    total = jnp.zeros((channels, height, breadth), jnp.float32)
    for tap_row in range(3):
        for tap_col in range(3):
            window = padded[:, tap_row : tap_row + height, tap_col : tap_col + breadth]
            total = total + jnp.einsum(
                "oc,chw->ohw", kernel[tap_row, tap_col], window, preferred_element_type=jnp.float32
            )
    land = jnp.broadcast_to(
        own_live.astype(jnp.float32).reshape(PR, 1, PC, 1), (PR, 16, PC, 16)
    ).reshape(height, breadth)
    return ((total + bias[:, None, None]) * land[None]).astype(jnp.bfloat16)


def solution(mesh):
    placed = (P(("lat", "lon"), None), P(), P(), P(), P(), P(), P())
    return jax.shard_map(
        per_device, mesh=mesh, in_specs=placed, out_specs=P(None, "lat", "lon"), check_vma=False
    )
```

profile of v0, /device:TPU:40, one launch (start us, length us, event | category | flops | bytes accessed | tf_op | source)
XLA Modules:
  0.0 211.6 jit_solution(3933851844532241639)
XLA Ops:
  0.0 0.9 add_select_fusion
  1.0 1.0 compare_and_fusion
  2.0 3.8 %convert_reduce_fusion = s32[128,144]{0,1:T(8,128)S(1)} fusion(s32[128,144]{0,1:T(8,128)S(1)} %get-tuple-element.7, pred[144,144]{1,0:T(8,128)(4,1)S(1)} %iota_compare_fusion.1, pred[128,144]{0,1:T(8,128)(4,1)S(1)} %get-tuple-element.6), kind=kLoop, calls=%fused_computation.10 | loop fusion | flops 13252608 | bytes 186624 | tf_op jit(solution)/shard_map/reduce_sum | solution.py:34
  5.7 1.1 select_reduce_fusion.1
  7.1 0.2 reshape.156
  7.3 1.8 concatenate.23
  9.2 2.2 %gather_fusion = bf16[384,1104]{1,0:T(8,128)(2,1)S(1)} fusion(bf16[961,1104]{1,0:T(8,128)(2,1)S(1)} %concatenate.23, s32[1024]{0:T(1024)S(1)} %get-tuple-element.13), kind=kCustom, calls=%fused_computation | custom fusion | bytes 1697280 | tf_op jit(solution)/shard_map/gather | solution.py:55
  11.4 1.3 reshape.155
  12.7 10.5 %all-to-all-start = ((bf16[128,3,1104]{2,1,0:T(4,128)(2,1)}), bf16[128,3,1104]{2,1,0:T(4,128)(2,1)S(1)}, u32[]{:S(2)}, u32[]{:S(2)}) async-start(bf16[128,3,1104]{2,1,0:T(4,128)(2,1)} %reshape.155), calls=%async_computation | async-start | bytes 2359296 | tf_op jit(solution)/shard_map/all_to_all | solution.py:56
  23.1 0.2 fusion.24
  23.5 0.2 convert_reduce_fusion.1
  23.9 0.1 broadcast_in_dim.22
  24.1 0.3 mul.71
  24.4 2.4 %broadcast_multiply_fusion = bf16[8,16,16,8,16]{4,3,2,1,0:T(8,128)(2,1)} fusion(bf16[16,16,16]{2,1,0:T(8,128)(2,1)S(1)} %mul.67, bf16[8,8]{1,0:T(8,128)(2,1)S(1)} %fusion.44), kind=kLoop, calls=%fused_computation.35 | loop fusion | flops 262144 | bytes 532608 | tf_op jit(solution)/shard_map/mul | solution.py:72
  26.8 8.8 %mul.70 = bf16[128,2048]{1,0:T(8,128)(2,1)} reshape(bf16[8,16,16,8,16]{4,3,2,1,0:T(8,128)(2,1)} %broadcast_multiply_fusion) | data formatting | bytes 1048576 | tf_op jit(solution)/shard_map/mul | solution.py:72
  35.6 6.6 %all-to-all-done = bf16[128,3,1104]{2,1,0:T(4,128)(2,1)S(1)} async-done(((bf16[128,3,1104]{2,1,0:T(4,128)(2,1)}), bf16[128,3,1104]{2,1,0:T(4,128)(2,1)S(1)}, u32[]{:S(2)}, u32[]{:S(2)}) %all-to-all-start) | async-done | bytes 847904 | tf_op jit(solution)/shard_map/all_to_all | solution.py:56
  42.2 3.2 %reshape_reshape.3 = bf16[6144,69]{1,0:T(8,128)(2,1)S(1)} reshape(bf16[128,3,1104]{2,1,0:T(4,128)(2,1)S(1)} %all-to-all-done) | data formatting | bytes 1695744 | tf_op jit(solution)/shard_map/reshape;reshape | solution.py:25
  45.5 0.7 convolution_convert_fusion.1
  46.1 0.9 copy.74
  47.0 1.1 reshape.150
  48.1 0.9 gather_fusion.1
  49.0 0.4 reshape.151
  49.4 1.2 copy.76
  50.7 1.5 multiply_bitcast_fusion
  52.1 4.1 %reshape.152 = bf16[1152,128]{0,1:T(8,128)(2,1)S(1)} reshape(bf16[64,18,8,16]{1,0,3,2:T(8,128)(2,1)} %multiply_bitcast_fusion) | data formatting | bytes 589824 | tf_op jit(solution)/shard_map/reshape | solution.py:68
  56.2 3.6 %convolution_convert_fusion = bf16[1152,2048]{1,0:T(8,128)(2,1)} fusion(bf16[1152,128]{0,1:T(8,128)(2,1)S(1)} %reshape.152, bf16[128,2048]{1,0:T(8,128)(2,1)S(1)} %copy-done.7), kind=kOutput, calls=%fused_computation.12 | convolution fusion | flops 606339072 | bytes 5537792 | tf_op jit(solution)/shard_map/dot_general | solution.py:74
  59.8 8.3 %reshape.153 = bf16[64,288,128]{2,1,0:T(8,128)(2,1)} reshape(bf16[1152,2048]{1,0:T(8,128)(2,1)} %convolution_convert_fusion) | data formatting | bytes 9437184 | tf_op jit(solution)/shard_map/reshape | solution.py:75
  68.1 4.3 %copy.77 = bf16[64,288,128]{2,0,1:T(8,128)(2,1)S(1)} copy(bf16[64,288,128]{2,1,0:T(8,128)(2,1)} %reshape.153) | data formatting | bytes 9437184 | tf_op jit(solution)/shard_map/reshape | solution.py:75
  72.5 1.9 collective-permute-start
  74.4 3.9 %collective-permute-start.1 = (bf16[64,1,128]{2,0,1:T(8,128)(2,1)S(1)}, bf16[64,1,128]{2,0,1:T(8,128)(2,1)S(1)}, u32[]{:S(2)}, u32[]{:S(2)}) collective-permute-start(bf16[64,1,128]{2,0,1:T(8,128)(2,1)S(1)} %get-tuple-element.11), channel_id=1, source_target_pairs={{16,0},{32,16},{48,32},{64,48},{80,64},{96,80},{112,96},{17,1},{33... | collective-permute-start | bytes 49160 | tf_op jit(solution)/shard_map/ppermute | solution.py:18
  78.3 5.4 %fusion.29 = f32[288,128,64]{1,2,0:T(8,128)} fusion(bf16[3,3,64,64]{3,2,1,0:T(8,128)(2,1)S(1)} %copy-done.9, bf16[64,288,128]{2,1,0:T(8,128)(2,1)S(1)} %copy-done.5), kind=kOutput, calls=%fused_computation.57 | convolution fusion | flops 301989888 | bytes 14172160 | tf_op jit(solution)/shard_map/oc,chw->ohw/dot_general | solution.py:81
  83.7 2.1 %constant_dynamic-update-slice_fusion.1 = bf16[64,290,128]{2,0,1:T(8,128)(2,1)S(1)} fusion(bf16[64,290,128]{2,0,1:T(8,128)(2,1)S(1)} %constant_dynamic-update-slice_fusion.2, bf16[64,288,128]{2,1,0:T(8,128)(2,1)S(1)} %copy-done.5), kind=kLoop, calls=%fused_computation.73 | loop fusion | bytes 9437184
  85.8 6.2 %fusion.54 = (bf16[64,290,1]{2,0,1:T(8,128)(2,1)}, bf16[64,290,1]{2,0,1:T(8,128)(2,1)}) fusion(bf16[64,290,128]{2,0,1:T(8,128)(2,1)S(1)} %constant_dynamic-update-slice_fusion), kind=kLoop, calls=%fused_computation.90 | loop fusion | bytes 148480 | tf_op jit(solution)/shard_map/slice | solution.py:18
  92.0 5.8 %copy.83 = bf16[64,290,1]{1,0,2:T(8,128)(2,1)S(1)} copy(bf16[64,290,1]{2,0,1:T(8,128)(2,1)} %get-tuple-element.8) | data formatting | bytes 74240 | tf_op jit(solution)/shard_map/slice | solution.py:18
  97.8 5.8 %copy.80 = bf16[64,290,1]{1,0,2:T(8,128)(2,1)S(1)} copy(bf16[64,290,1]{2,0,1:T(8,128)(2,1)} %get-tuple-element.9) | data formatting | bytes 74240 | tf_op jit(solution)/shard_map/slice | solution.py:16
  103.6 2.8 %collective-permute-start.2 = (bf16[64,290,1]{1,0,2:T(8,128)(2,1)S(1)}, bf16[64,290,1]{1,0,2:T(8,128)(2,1)S(1)}, u32[]{:S(2)}, u32[]{:S(2)}) collective-permute-start(bf16[64,290,1]{1,0,2:T(8,128)(2,1)S(1)} %copy.80), channel_id=1, source_target_pairs={{0,1},{1,2},{2,3},{3,4},{4,5},{5,6},{6,7},{7,8},{8,9},{9,10},{10,1... | collective-permute-start | bytes 111368 | tf_op jit(solution)/shard_map/ppermute | solution.py:15
  106.5 5.4 %collective-permute-start.3 = (bf16[64,290,1]{1,0,2:T(8,128)(2,1)S(1)}, bf16[64,290,1]{1,0,2:T(8,128)(2,1)S(1)}, u32[]{:S(2)}, u32[]{:S(2)}) collective-permute-start(bf16[64,290,1]{1,0,2:T(8,128)(2,1)S(1)} %copy.83), channel_id=1, source_target_pairs={{1,0},{2,1},{3,2},{4,3},{5,4},{6,5},{7,6},{8,7},{9,8},{10,9},{11,1... | collective-permute-start | bytes 111368 | tf_op jit(solution)/shard_map/ppermute | solution.py:18
  111.9 7.3 %fusion.14 = f32[288,128,64]{1,2,0:T(8,128)} fusion(bf16[64,1,128]{2,0,1:T(8,128)(2,1)S(1)} %collective-permute-done.1, bf16[64,288,128]{2,0,1:T(8,128)(2,1)} %copy-done.6, bf16[3,3,64,64]{3,2,1,0:T(8,128)(2,1)S(1)} %copy-done.9), kind=kOutput, calls=%fused_computation.26 | convolution fusion | flops 311427072 | bytes 14188544 | tf_op jit(solution)/shard_map/oc,chw->ohw/dot_general | solution.py:81
  119.2 5.1 %fusion.18 = f32[288,128,64]{1,2,0:T(8,128)} fusion(bf16[64,288,128]{2,0,1:T(8,128)(2,1)S(1)} %bitcast.72, bf16[64,1,128]{2,0,1:T(8,128)(2,1)S(1)} %collective-permute-done, bf16[3,3,64,64]{3,2,1,0:T(8,128)(2,1)S(1)} %copy-done.9), kind=kOutput, calls=%fused_computation.32 | convolution fusion | flops 311427072 | bytes 14188544 | tf_op jit(solution)/shard_map/oc,chw->ohw/dot_general | solution.py:81
  124.3 6.5 %copy.81 = bf16[64,290,1]{2,0,1:T(8,128)(2,1)} copy(bf16[64,290,1]{1,0,2:T(8,128)(2,1)S(1)} %collective-permute-done.2) | data formatting | bytes 74240 | tf_op jit(solution)/shard_map/ppermute | solution.py:15
  130.8 9.9 %fusion.10 = f32[288,128,64]{1,2,0:T(8,128)} fusion(bf16[64,290,1]{2,0,1:T(8,128)(2,1)} %copy.81, bf16[64,290,128]{2,0,1:T(8,128)(2,1)} %copy-done.2, bf16[3,3,64,64]{3,2,1,0:T(8,128)(2,1)S(1)} %copy-done.9), kind=kOutput, calls=%fused_computation.21 | convolution fusion | flops 311427072 | bytes 14242048 | tf_op jit(solution)/shard_map/oc,chw->ohw/dot_general | solution.py:81
  140.8 5.0 %fusion.16 = f32[288,128,64]{1,2,0:T(8,128)} fusion(bf16[64,290,128]{2,0,1:T(8,128)(2,1)S(1)} %bitcast.68, bf16[64,290,1]{2,0,1:T(8,128)(2,1)S(1)} %copy-done.4, bf16[3,3,64,64]{3,2,1,0:T(8,128)(2,1)S(1)} %copy-done.9), kind=kOutput, calls=%fused_computation.29 | convolution fusion | flops 311427072 | bytes 18956288 | tf_op jit(solution)/shard_map/oc,chw->ohw/dot_general | solution.py:81
  145.7 4.8 %fusion.7 = f32[288,128,64]{1,2,0:T(8,128)} fusion(bf16[64,290,1]{2,0,1:T(8,128)(2,1)S(1)} %copy-done.4, bf16[64,290,128]{2,0,1:T(8,128)(2,1)S(1)} %bitcast.68, bf16[3,3,64,64]{3,2,1,0:T(8,128)(2,1)S(1)} %copy-done.9), kind=kOutput, calls=%fused_computation.19 | convolution fusion | flops 311427072 | bytes 18956288 | tf_op jit(solution)/shard_map/oc,chw->ohw/dot_general | solution.py:81
  150.6 6.1 %copy.84 = bf16[64,290,1]{2,0,1:T(8,128)(2,1)} copy(bf16[64,290,1]{1,0,2:T(8,128)(2,1)S(1)} %collective-permute-done.3) | data formatting | bytes 74240 | tf_op jit(solution)/shard_map/ppermute | solution.py:18
  156.7 10.6 %fusion.4 = f32[288,128,64]{1,2,0:T(8,128)} fusion(bf16[64,290,128]{2,0,1:T(8,128)(2,1)} %copy-done.2, bf16[64,290,1]{2,0,1:T(8,128)(2,1)} %copy.84, bf16[3,3,64,64]{3,2,1,0:T(8,128)(2,1)S(1)} %copy-done.9), kind=kOutput, calls=%fused_computation.17 | convolution fusion | flops 311427072 | bytes 14242048 | tf_op jit(solution)/shard_map/oc,chw->ohw/dot_general | solution.py:81
  167.3 5.5 %fusion.1 = f32[288,128,64]{1,2,0:T(8,128)} fusion(bf16[64,290,128]{2,0,1:T(8,128)(2,1)S(1)} %bitcast.70, bf16[64,290,1]{2,0,1:T(8,128)(2,1)S(1)} %copy-done.3, bf16[3,3,64,64]{3,2,1,0:T(8,128)(2,1)S(1)} %copy-done.9), kind=kOutput, calls=%fused_computation.15 | convolution fusion | flops 311427072 | bytes 18956288 | tf_op jit(solution)/shard_map/oc,chw->ohw/dot_general | solution.py:81
  172.7 31.1 %fusion.20 = bf16[64,288,128]{2,0,1:T(8,128)(2,1)} fusion(f32[288,128]{1,0:T(8,128)S(1)} %mul.71, f32[64]{0:T(128)S(1)} %copy-done.11, f32[288,128,64]{1,2,0:T(8,128)} %fusion.14, f32[288,128,64]{1,2,0:T(8,128)} %fusion.16, f32[288,128,64]{1,2,0:T(8,128)} %fusion.1, f32[288,128,64]{1,2,0:T(8,128)} %fusion.29, f32[288,128,64]{1,2,0:T(8,128)} %fusion.7, ...), kind=kOutput, calls=%fused_computation.34 | convolution fusion | flops 337379328 | bytes 85168896 | tf_op jit(solution)/shard_map/oc,chw->ohw/dot_general | solution.py:81
  203.8 7.6 %copy.87 = bf16[64,288,128]{2,1,0:T(8,128)(2,1)} copy(bf16[64,288,128]{2,0,1:T(8,128)(2,1)} %fusion.20) | data formatting | bytes 9437184 | tf_op jit(solution)/shard_map/convert_element_type | solution.py:87
  (58 shorter events, 0.8 us)
Async XLA Ops:
  0.0 45.5 %copy-start = (bf16[69,64]{0,1:T(8,128)(2,1)S(1)}, bf16[69,64]{0,1:T(8,128)(2,1)}, u32[]{:S(2)}) copy-start(bf16[69,64]{0,1:T(8,128)(2,1)} %param.8) | copy-start | bytes 26500
  9.1 14.0 %copy-start.8 = (s32[128,144]{0,1:T(8,128)S(1)}, s32[128,144]{0,1:T(8,128)}, u32[]{:S(2)}) copy-start(s32[128,144]{0,1:T(8,128)} %param.13) | copy-start | bytes 221188
  9.2 14.7 %copy-start.10 = (bf16[16,256]{1,0:T(8,128)(2,1)S(1)}, bf16[16,256]{1,0:T(8,128)(2,1)}, u32[]{:S(2)}) copy-start(bf16[16,256]{1,0:T(8,128)(2,1)} %param.9) | copy-start | bytes 24580
  12.7 29.6 %all-to-all-start = ((bf16[128,3,1104]{2,1,0:T(4,128)(2,1)}), bf16[128,3,1104]{2,1,0:T(4,128)(2,1)S(1)}, u32[]{:S(2)}, u32[]{:S(2)}) async-start(bf16[128,3,1104]{2,1,0:T(4,128)(2,1)} %reshape.155), calls=%async_computation | async-start | bytes 2359296 | tf_op jit(solution)/shard_map/all_to_all | solution.py:56
  49.4 6.8 %copy-start.7 = (bf16[128,2048]{1,0:T(8,128)(2,1)S(1)}, bf16[128,2048]{1,0:T(8,128)(2,1)}, u32[]{:S(2)}) copy-start(bf16[128,2048]{1,0:T(8,128)(2,1)} %mul.70) | copy-start | bytes 1572868
  68.1 10.1 %copy-start.5 = (bf16[64,288,128]{2,1,0:T(8,128)(2,1)S(1)}, bf16[64,288,128]{2,1,0:T(8,128)(2,1)}, u32[]{:S(2)}) copy-start(bf16[64,288,128]{2,1,0:T(8,128)(2,1)} %reshape.153) | copy-start | bytes 14155780
  68.1 10.1 %copy-start.9 = (bf16[3,3,64,64]{3,2,1,0:T(8,128)(2,1)S(1)}, bf16[3,3,64,64]{3,2,1,0:T(8,128)(2,1)}, u32[]{:S(2)}) copy-start(bf16[3,3,64,64]{3,2,1,0:T(8,128)(2,1)} %param.10) | copy-start | bytes 221188
  72.5 11.2 %copy-start.6 = (bf16[64,288,128]{2,0,1:T(8,128)(2,1)}, bf16[64,288,128]{2,0,1:T(8,128)(2,1)S(1)}, u32[]{:S(2)}) copy-start(bf16[64,288,128]{2,0,1:T(8,128)(2,1)S(1)} %copy.77) | copy-start | bytes 14155780
  72.5 11.2 %collective-permute-start = (bf16[64,1,128]{2,0,1:T(8,128)(2,1)S(1)}, bf16[64,1,128]{2,0,1:T(8,128)(2,1)S(1)}, u32[]{:S(2)}, u32[]{:S(2)}) collective-permute-start(bf16[64,1,128]{2,0,1:T(8,128)(2,1)S(1)} %get-tuple-element.10), channel_id=1, source_target_pairs={{0,16},{16,32},{32,48},{48,64},{64,80},{80,96},{96,112},{1,17},{17... | collective-permute-start | bytes 49160 | tf_op jit(solution)/shard_map/ppermute | solution.py:15
  74.4 11.4 %collective-permute-start.1 = (bf16[64,1,128]{2,0,1:T(8,128)(2,1)S(1)}, bf16[64,1,128]{2,0,1:T(8,128)(2,1)S(1)}, u32[]{:S(2)}, u32[]{:S(2)}) collective-permute-start(bf16[64,1,128]{2,0,1:T(8,128)(2,1)S(1)} %get-tuple-element.11), channel_id=1, source_target_pairs={{16,0},{32,16},{48,32},{64,48},{80,64},{96,80},{112,96},{17,1},{33... | collective-permute-start | bytes 49160 | tf_op jit(solution)/shard_map/ppermute | solution.py:18
  85.8 6.2 %copy-start.2 = (bf16[64,290,128]{2,0,1:T(8,128)(2,1)}, bf16[64,290,128]{2,0,1:T(8,128)(2,1)S(1)}, u32[]{:S(2)}) copy-start(bf16[64,290,128]{2,0,1:T(8,128)(2,1)S(1)} %constant_dynamic-update-slice_fusion) | copy-start | bytes 14254084
  97.8 21.5 %slice-start.4 = ((s8[4718592]{0:T(1024)(128)(4,1)}), s8[524288]{0:T(1024)(128)(4,1)S(1)}, s32[]{:S(2)}) async-start(s8[4718592]{0:T(1024)(128)(4,1)} %bitcast.71), calls=%async_computation.5 | async-start | bytes 1048576
  103.6 15.6 %slice-start.5 = ((s8[4718592]{0:T(1024)(128)(4,1)}), s8[4194304]{0:T(1024)(128)(4,1)S(1)}, s32[]{:S(2)}) async-start(s8[4718592]{0:T(1024)(128)(4,1)} %bitcast.71), calls=%async_computation.6 | async-start | bytes 8388608
  103.6 20.7 %collective-permute-start.2 = (bf16[64,290,1]{1,0,2:T(8,128)(2,1)S(1)}, bf16[64,290,1]{1,0,2:T(8,128)(2,1)S(1)}, u32[]{:S(2)}, u32[]{:S(2)}) collective-permute-start(bf16[64,290,1]{1,0,2:T(8,128)(2,1)S(1)} %copy.80), channel_id=1, source_target_pairs={{0,1},{1,2},{2,3},{3,4},{4,5},{5,6},{6,7},{7,8},{8,9},{9,10},{10,1... | collective-permute-start | bytes 111368 | tf_op jit(solution)/shard_map/ppermute | solution.py:15
  106.5 44.1 %collective-permute-start.3 = (bf16[64,290,1]{1,0,2:T(8,128)(2,1)S(1)}, bf16[64,290,1]{1,0,2:T(8,128)(2,1)S(1)}, u32[]{:S(2)}, u32[]{:S(2)}) collective-permute-start(bf16[64,290,1]{1,0,2:T(8,128)(2,1)S(1)} %copy.83), channel_id=1, source_target_pairs={{1,0},{2,1},{3,2},{4,3},{5,4},{6,5},{7,6},{8,7},{9,8},{10,9},{11,1... | collective-permute-start | bytes 111368 | tf_op jit(solution)/shard_map/ppermute | solution.py:18
  124.3 16.4 %slice-start = ((s8[4751360]{0:T(1024)(128)(4,1)}), s8[557056]{0:T(1024)(128)(4,1)S(1)}, s32[]{:S(2)}) async-start(s8[4751360]{0:T(1024)(128)(4,1)} %bitcast.67), calls=%async_computation.1 | async-start | bytes 1114112
  130.8 9.9 %slice-start.1 = ((s8[4751360]{0:T(1024)(128)(4,1)}), s8[4194304]{0:T(1024)(128)(4,1)S(1)}, s32[]{:S(2)}) async-start(s8[4751360]{0:T(1024)(128)(4,1)} %bitcast.67), calls=%async_computation.2 | async-start | bytes 8388608
  130.8 9.9 %copy-start.4 = (bf16[64,290,1]{2,0,1:T(8,128)(2,1)S(1)}, bf16[64,290,1]{2,0,1:T(8,128)(2,1)}, u32[]{:S(2)}) copy-start(bf16[64,290,1]{2,0,1:T(8,128)(2,1)} %copy.81) | copy-start | bytes 111364
  150.6 16.7 %slice-start.2 = ((s8[4751360]{0:T(1024)(128)(4,1)}), s8[557056]{0:T(1024)(128)(4,1)S(1)}, s32[]{:S(2)}) async-start(s8[4751360]{0:T(1024)(128)(4,1)} %bitcast.69), calls=%async_computation.3 | async-start | bytes 1114112
  156.7 10.6 %slice-start.3 = ((s8[4751360]{0:T(1024)(128)(4,1)}), s8[4194304]{0:T(1024)(128)(4,1)S(1)}, s32[]{:S(2)}) async-start(s8[4751360]{0:T(1024)(128)(4,1)} %bitcast.69), calls=%async_computation.4 | async-start | bytes 8388608
  156.7 10.6 %copy-start.3 = (bf16[64,290,1]{2,0,1:T(8,128)(2,1)S(1)}, bf16[64,290,1]{2,0,1:T(8,128)(2,1)}, u32[]{:S(2)}) copy-start(bf16[64,290,1]{2,0,1:T(8,128)(2,1)} %copy.84) | copy-start | bytes 111364
  167.3 5.5 %copy-start.11 = (f32[64]{0:T(128)S(1)}, f32[64]{0:T(128)}, u32[]{:S(2)}) copy-start(f32[64]{0:T(128)} %param.11) | copy-start | bytes 772
  172.7 38.6 %copy-start.1 = (bf16[69,64]{0,1:T(8,128)(2,1)S(1)}, bf16[69,64]{0,1:T(8,128)(2,1)}, u32[]{:S(2)}) copy-start(bf16[69,64]{0,1:T(8,128)(2,1)} %param.8) | copy-start | bytes 26500
where the time goes:
time: 215 us; the launch traced here: 212 us
  matrix products  88.8 us (41%)
  local copies, waits for them, and re-layouts  79.9 us (37%)
  starting transfers between devices  24.5 us (11%)
  other arithmetic  11.2 us (5%)
  waiting for transfers between devices  6.63 us (3%)
    dot_general x9, matrix products, per_device(): jnp.einsum('oc,chw->ohw', kernel[tap_row, tap_col], window, preferred_ele...  84.6 us
    reshape x2, local copies, waits for them, and re-layouts, per_device(): image = image.reshape(channels, height, breadth)  12.6 us
    slice x2, local copies, waits for them, and re-layouts, with_halo(): lax.slice_in_dim(block, 0, width, axis=dim)  11.9 us
    all_to_all x1, starting transfers between devices, per_device(): lax.all_to_all(outgoing, ('lat', 'lon'), split_axis=0, concat_axis=0, til...  10.5 us
    ppermute x2, starting transfers between devices, with_halo(): lax.ppermute(lax.slice_in_dim(block, 0, width, axis=dim), axis, backward)  9.22 us
    mul x2, local copies, waits for them, and re-layouts, per_device(): spread = same_col[:, None, None, :, None] * cells[None, :, :, None, :]  8.92 us
    convert_element_type x1, local copies, waits for them, and re-layouts, per_device(): return ((total + bias[:, None, None]) * land[None]).astype(jnp.bfloat16)  7.56 us
    all_to_all x1, waiting for transfers between devices, per_device(): lax.all_to_all(outgoing, ('lat', 'lon'), split_axis=0, concat_axis=0, til...  6.62 us
  transfers between devices with their start and end apart: 5, of which 1 were waited for; matrix products, arithmetic and copies ran while one was open for 28% of the time, Pallas kernels for 0%

commit v1 on v0

v1 whole, which is shorter than its diff:
```python
import jax
import jax.numpy as jnp
from jax import lax
from jax.experimental import pallas as pl
from jax.experimental.pallas import tpu as pltpu
from jax.sharding import PartitionSpec as P

PR = 18
PC = 8
CELLS = 16
WR = PR + 2
WC = PC + 2
MOST = 3
CB_ROWS = 24
CB_COLS = 40
HELD_ROWS = 20
C_IN = 69
C = 64
GRID_COLS = 640


def pack_body(ids_ref, coarse_ref, w_ref, out_ref, raw, weights, mixed, sems):
    n_lat, n_lon = 8, 16
    a = lax.axis_index("lat")
    b = lax.axis_index("lon")
    first = ids_ref[0, 0]
    owner = first // (CB_ROWS * CB_COLS)
    local = first % (CB_ROWS * CB_COLS)
    r0 = (local // CB_COLS) * n_lat + owner // n_lon
    c0 = (local % CB_COLS) * n_lon + owner % n_lon
    low = jnp.clip((r0 + 7) // 8 - 1, 0, CB_ROWS - HELD_ROWS)
    c_first = c0 - 1 + (b - c0 + 1 + 16 * CB_COLS) % n_lon
    lc_first = ((c_first + GRID_COLS) % GRID_COLS) // n_lon
    tile0 = lc_first // 8
    tile1 = (tile0 + 1) % (CB_COLS // 8)
    copies = []
    for slot, tile in ((0, tile0), (1, tile1)):
        copy = pltpu.make_async_copy(
            coarse_ref.at[pl.ds(low, HELD_ROWS), pl.ds(pl.multiple_of(tile * 8, 8), 8), :],
            raw.at[slot],
            sems.at[slot],
        )
        copy.start()
        copies.append(copy)
    w = w_ref[...].astype(jnp.float32)
    weights[...] = jnp.zeros_like(weights)
    for j in range(8):
        weights[j, 10 * j : 10 * j + C_IN, 0:C] = w
        weights[j, 10 * j + C_IN : 10 * j + 2 * C_IN, C : 2 * C] = w
    for copy in copies:
        copy.wait()
    count = 2 * HELD_ROWS * 8
    for j in range(8):
        width = min(256, CELLS * C_IN - 128 * j)
        rows = raw[:, :, :, 128 * j : 128 * j + width].reshape(count, width)
        part = jnp.dot(
            rows, weights[j, 0:width, :].astype(jnp.bfloat16), preferred_element_type=jnp.float32
        )
        mixed[pl.ds(j, count, stride=8), :] = part
    starts = []
    for i in range(n_lat):
        top = r0 + PR * i - 1
        r_first = top + (a - top + 512) % n_lat
        lr = (r_first + 8) // 8 - 1 - low
        for m in range(MOST):
            starts.append(jnp.clip(lr + m, 0, HELD_ROWS - 1) * 8)

    def one_column(j, carry):
        left = c0 + PC * j - 1
        d = (b - left + 16 * CB_COLS) % n_lon
        n = (left + d - c_first) // n_lon
        pos = jnp.minimum(lc_first % 8 + n, 15)
        base = (pos // 8) * (HELD_ROWS * 8) + pos % 8
        for i in range(n_lat):
            for m in range(MOST):
                at = (base + starts[i * MOST + m]) * 8
                block = mixed[pl.ds(pl.multiple_of(at, 8), 8), :]
                out_ref[(i * n_lon + j) * MOST + m] = block.astype(jnp.bfloat16)
        return carry

    lax.fori_loop(0, n_lon, one_column, 0)


def pack(block_ids, coarse, w_mix):
    return pl.pallas_call(
        pack_body,
        out_shape=jax.ShapeDtypeStruct((128 * MOST, 8, 128), jnp.bfloat16),
        grid=(1,),
        in_specs=[
            pl.BlockSpec((8, 128), lambda g: (0, 0), memory_space=pltpu.SMEM),
            pl.BlockSpec(memory_space=pl.ANY),
            pl.BlockSpec((C_IN, C), lambda g: (0, 0)),
        ],
        out_specs=pl.BlockSpec((128 * MOST, 8, 128), lambda g: (0, 0, 0)),
        scratch_shapes=[
            pltpu.VMEM((2, HELD_ROWS, 8, CELLS * C_IN), jnp.bfloat16),
            pltpu.VMEM((8, 256, 2 * C), jnp.float32),
            pltpu.VMEM((2 * HELD_ROWS * 8 * 8, 128), jnp.float32),
            pltpu.SemaphoreType.DMA((2,)),
        ],
        name="pack",
    )(block_ids, coarse.reshape(CB_ROWS, CB_COLS, CELLS * C_IN), w_mix)


def fine_body(where_ref, inc_ref, spread_ref, taps_ref, bias_ref, land_ref, out_ref, cells, cells_t, field):
    step = pl.program_id(0)

    @pl.when(step == 0)
    def _():
        lane = lax.broadcasted_iota(jnp.int32, (8, 128), 1)
        lower = lane < C

        def pair_of_rows(q, carry):
            for col in range(WC):
                got = []
                for half in range(2):
                    at = where_ref[(2 * q + half) * WC + col]
                    block = inc_ref[jnp.maximum(at, 0)].astype(jnp.float32)
                    got.append(jnp.where(at >= 0, block, 0.0))
                u, v = got
                cells[8 * col : 8 * col + 8, :] = jnp.where(lower, u, pltpu.roll(v, C, 1))
                cells[8 * (WC + col) : 8 * (WC + col) + 8, :] = jnp.where(lower, pltpu.roll(u, C, 1), v)
            cells_t[pl.ds(pl.multiple_of(q * 128, 128), 128), :] = cells[...].T.astype(jnp.bfloat16)
            return carry

        cells[8 * 2 * WC :, :] = jnp.zeros((256 - 16 * WC, 128), jnp.float32)
        lax.fori_loop(0, WR // 2, pair_of_rows, 0)

        def upsample(n, carry):
            right = jnp.concatenate([spread_ref[2 * n], spread_ref[2 * n + 1]], axis=1)
            fine = jnp.dot(
                cells_t[:, 0 : CELLS * WC], right, preferred_element_type=jnp.float32
            ).astype(jnp.bfloat16)
            tap = n // 8
            row = 2 * (n % 8)
            field[tap, :, row] = fine[:, 0:128].reshape(WR, C, 128)
            field[tap, :, row + 1] = fine[:, 128:256].reshape(WR, C, 128)
            return carry

        lax.fori_loop(0, 24, upsample, 0)

    sub = lax.broadcasted_iota(jnp.int32, (32, 8, 128), 1)
    land = land_ref[pl.ds(step, 1), :]
    even = []
    odd = []
    for h in range(2):
        quads = []
        for q in range(2):
            blocks = []
            for tap in range(3):
                for rr in range(6):
                    row = 15 + 4 * (2 * h + q) + rr
                    blocks.append(field[tap, step + row // 16, row % 16])
            quads.append(jnp.concatenate(blocks, axis=0))
        right = jnp.concatenate(quads, axis=1)
        total = jnp.dot(taps_ref[...], right, preferred_element_type=jnp.float32)
        left = ((total[:, 0:128] + bias_ref[...]) * land).reshape(32, 8, 128)
        other = ((total[:, 128:256] + bias_ref[...]) * land).reshape(32, 8, 128)
        even.append(jnp.where(sub < 4, left, pltpu.roll(other, 4, 1)))
        odd.append(jnp.where(sub < 4, pltpu.roll(left, 4, 1), other))
    out_ref[:, 0] = jnp.concatenate(even, axis=1).astype(jnp.bfloat16)
    out_ref[:, 1] = jnp.concatenate(odd, axis=1).astype(jnp.bfloat16)


def fine(where, incoming, spread, taps, bias_rows, land):
    return pl.pallas_call(
        fine_body,
        out_shape=jax.ShapeDtypeStruct((C // 2, 2, PR * 16, 128), jnp.bfloat16),
        grid=(PR,),
        in_specs=[
            pl.BlockSpec(memory_space=pltpu.SMEM),
            pl.BlockSpec((128 * MOST, 8, 128), lambda g: (0, 0, 0), pipeline_mode=pl.Buffered(1)),
            pl.BlockSpec((48, CELLS * WC, 128), lambda g: (0, 0, 0), pipeline_mode=pl.Buffered(1)),
            pl.BlockSpec((4 * C, 18 * C), lambda g: (0, 0), pipeline_mode=pl.Buffered(1)),
            pl.BlockSpec((4 * C, 128), lambda g: (0, 0), pipeline_mode=pl.Buffered(1)),
            pl.BlockSpec((PR, 128), lambda g: (0, 0), pipeline_mode=pl.Buffered(1)),
        ],
        out_specs=pl.BlockSpec((C // 2, 2, 16, 128), lambda g: (0, 0, g, 0)),
        scratch_shapes=[
            pltpu.VMEM((256, 128), jnp.float32),
            pltpu.VMEM((WR * C, 256), jnp.bfloat16),
            pltpu.VMEM((3, WR, 16, C, 128), jnp.bfloat16),
        ],
        name="fine",
    )(where, incoming, spread, taps, bias_rows, land)


def spread_of(interp):
    cells = interp.reshape(8, 2, 16, 16).transpose(2, 1, 0, 3)
    wide = jnp.tile(cells, (1, 1, 1, WC))
    shifted = jnp.stack([wide[..., 15 + tap : 143 + tap] for tap in range(3)])
    tap = jnp.arange(3)[:, None, None]
    column = (jnp.arange(128)[None, None, :] + tap + 15) // 16
    same = column == jnp.arange(WC)[None, :, None]
    full = jnp.where(same[:, None, None, :, None, :], shifted[:, :, :, None], 0)
    return full.reshape(48, CELLS * WC, 128).astype(jnp.bfloat16)


def taps_of(kernel):
    by = kernel.transpose(2, 1, 0, 3)
    rows = [jnp.pad(by, ((0, 0), (0, 0), (r, 3 - r), (0, 0))) for r in range(4)]
    return jnp.stack(rows, axis=1).reshape(4 * C, 18 * C)


def per_device(coarse, w_mix, interp, kernel, bias, block_ids, valid):
    n_lat, n_lon = 8, 16
    i = lax.axis_index("lat")
    j = lax.axis_index("lon")
    outgoing = pack(block_ids, coarse, w_mix)
    incoming = lax.all_to_all(outgoing, ("lat", "lon"), split_axis=0, concat_axis=0, tiled=True)
    first = block_ids[0, 0]
    owner = first // (CB_ROWS * CB_COLS)
    local = first % (CB_ROWS * CB_COLS)
    r0 = (local // CB_COLS) * n_lat + owner // n_lon
    c0 = (local % CB_COLS) * n_lon + owner % n_lon
    grid = valid.reshape(n_lat, n_lon, PR, PC).transpose(0, 2, 1, 3).reshape(n_lat * PR, n_lon * PC)
    window = lax.dynamic_slice(jnp.pad(grid, 1), (i * PR, j * PC), (WR, WC))
    row = jnp.arange(WR)[:, None]
    col = jnp.arange(WC)[None, :]
    source = (r0 + PR * i - 1 + row + 8) % n_lat * n_lon + (c0 + PC * j - 1 + col + 16) % n_lon
    where = jnp.where(window > 0, source * MOST + row // 8, -1).reshape(WR * WC).astype(jnp.int32)
    own = window[1:-1, 1:-1].astype(jnp.float32)
    land = jnp.repeat(own, 16, axis=1)
    bias_rows = jnp.broadcast_to(jnp.repeat(bias, 4)[:, None], (4 * C, 128))
    out = fine(where, incoming, spread_of(interp), taps_of(kernel), bias_rows, land)
    return out.reshape(C, PR * 16, 128)


def solution(mesh):
    placed = (P(("lat", "lon"), None), P(), P(), P(), P(), P(), P())
    return jax.shard_map(
        per_device, mesh=mesh, in_specs=placed, out_specs=P(None, "lat", "lon"), check_vma=False
    )
```

time: 215 us -> 60.1 us (0.28)
  the two profiles are of different devices: /device:TPU:40 before, /device:TPU:1 now
where the time goes in v1:
time: 60.1 us; the launch traced here: 59.7 us
  Pallas kernels  27.4 us (46%)
  local copies, waits for them, and re-layouts  13 us (22%)
  starting transfers between devices  11.5 us (19%)
  waiting for transfers between devices  3.86 us (6%)
  other arithmetic  1.99 us (3%)
  between operations  1.97 us (3%)
    pallas_call x1, Pallas kernels, fine(): pl.pallas_call(fine_body, out_shape=jax.ShapeDtypeStruct((C // 2, 2, PR *...  23.2 us
    all_to_all x1, starting transfers between devices, per_device(): lax.all_to_all(outgoing, ('lat', 'lon'), split_axis=0, concat_axis=0, til...  11.5 us
    pallas_call x1, Pallas kernels, pack(): pl.pallas_call(pack_body, out_shape=jax.ShapeDtypeStruct((128 * MOST, 8,...  4.19 us
    all_to_all x1, waiting for transfers between devices, per_device(): lax.all_to_all(outgoing, ('lat', 'lon'), split_axis=0, concat_axis=0, til...  3.86 us
    unnamed x18, local copies, waits for them, and re-layouts  3.36 us
    reshape x1, local copies, waits for them, and re-layouts, taps_of(): return jnp.stack(rows, axis=1).reshape(4 * C, 18 * C)  1.71 us
    select_n x1, other arithmetic, spread_of(): full = jnp.where(same[:, None, None, :, None, :], shifted[:, :, :, None], 0)  1.42 us
    slice x1, local copies, waits for them, and re-layouts, per_device(): first = block_ids[0, 0]  1.2 us
  transfers between devices with their start and end apart: 1, of which 1 were waited for; matrix products, arithmetic and copies ran while one was open for 18% of the time, Pallas kernels for 0%

profile of v1, /device:TPU:1, one launch (start us, length us, event | category | flops | bytes accessed | tf_op | source)
XLA Modules:
  0.0 59.7 jit_solution(17301625574500781507)
XLA Ops:
  0.0 1.4 %copy.15.w_ref = bf16[69,64]{1,0:T(8,128)(2,1)} copy(bf16[69,64]{0,1:T(8,128)(2,1)} %param.8) | data formatting | bytes 17664 | tf_op args[1]
  1.4 1.6 %copy.14.ids_ref = s32[128,144]{1,0:T(8,128)} copy(s32[128,144]{0,1:T(8,128)} %param.12) | data formatting | bytes 147456 | tf_op args[5]
  3.0 4.2 %pack.1 = bf16[384,8,128]{2,1,0:T(8,128)(2,1)} custom-call(s32[128,144]{1,0:T(8,128)} %copy.14.ids_ref, bf16[24,40,1104]{2,1,0:T(8,128)(2,1)} %bitcast.31, bf16[69,64]{1,0:T(8,128)(2,1)} %copy.15.w_ref), custom_call_target="tpu_custom_call" | custom-call | tf_op jit(solution)/shard_map/pack/pallas_call | solution.py:85
  7.2 0.0 copy-start.6
  7.3 0.0 copy-start.5
  7.3 11.5 %all-to-all-start = ((bf16[384,8,128]{2,1,0:T(8,128)(2,1)}), bf16[384,8,128]{2,1,0:T(8,128)(2,1)S(1)}, u32[]{:S(2)}, u32[]{:S(2)}) async-start(bf16[384,8,128]{2,1,0:T(8,128)(2,1)} %pack.1), calls=%async_computation | async-start | bytes 1572864 | tf_op jit(solution)/shard_map/all_to_all | solution.py:210
  18.8 1.2 %slice.15 = s32[1,1]{0,1:T(1,128)} slice(s32[128,144]{0,1:T(8,128)} %param.12), slice={[0:1], [0:1]} | slice | bytes 8 | tf_op jit(solution)/shard_map/slice | solution.py:211
  21.8 0.0 copy-done.6
  21.8 0.1 reshape.185
  21.9 0.0 copy-done.5
  22.0 0.2 reshape.181
  22.2 0.7 %copy.12 = s32[8,18,16,8]{1,0,3,2:T(8,128)S(1)} copy(s32[8,18,16,8]{2,0,3,1:T(8,128)S(1)} %bitcast.30) | data formatting | bytes 147456 | tf_op jit(solution)/shard_map/transpose | solution.py:216
  22.9 0.2 reshape.182
  23.0 0.0 copy-start.4
  23.1 0.2 tile.4
  23.2 0.7 %tile.10 = bf16[16,2,8,160]{3,2,1,0:T(8,128)(2,1)S(1)} reshape(bf16[16,2,8,10,16]{4,3,2,1,0:T(8,128)(2,1)S(1)} %tile.4) | data formatting | bytes 163840 | tf_op jit(solution)/shard_map/tile | solution.py:190
  24.0 0.8 %slice_bitcast_fusion.2 = (bf16[1,16,2,8,128]{4,3,2,1,0:T(8,128)(2,1)}, bf16[1,16,2,8,128]{4,3,2,1,0:T(8,128)(2,1)}, bf16[1,16,2,8,128]{4,3,2,1,0:T(8,128)(2,1)}) fusion(bf16[16,2,8,160]{3,2,1,0:T(8,128)(2,1)S(1)} %tile.10), kind=kLoop, calls=%fused_computation.11 | loop fusion | bytes 393216 | tf_op jit(solution)/shard_map/stack | solution.py:191
  24.8 0.0 copy-done.4
  24.8 0.3 pad_bitcast_fusion.3
  25.0 0.1 add_select_fusion
  25.1 0.0 copy-start.7
  25.1 0.3 pad_maximum_fusion
  25.5 0.1 fusion.1
  25.5 0.2 copy-done.7
  25.8 0.1 broadcast_in_dim.48
  25.9 0.1 broadcast_in_dim.49
  26.0 0.1 copy.13
  26.1 0.7 %reshape.183.where_ref = s32[200]{0:T(256)} reshape(s32[20,10]{1,0:T(8,128)S(1)} %copy.13) | data formatting | bytes 1600 | tf_op jit(solution)/shard_map/reshape | solution.py:221
  26.8 0.1 copy.18
  26.8 0.1 broadcast_in_dim.51
  26.9 0.7 %reshape.187.land_ref = f32[18,128]{1,0:T(8,128)} reshape(f32[18,8,16]{2,1,0:T(8,128)S(1)} %broadcast_in_dim.51) | data formatting | bytes 18432 | tf_op jit(solution)/shard_map/reshape | solution.py:223
  27.6 0.8 %copy.17 = bf16[64,4,3,6,64]{4,3,2,1,0:T(8,128)(2,1)S(1)} copy(bf16[64,4,3,6,64]{4,0,2,3,1:T(8,128)(2,1)S(1)} %pad_maximum_fusion) | data formatting | bytes 1179648 | tf_op jit(solution)/shard_map/stack | solution.py:202
  28.4 0.0 copy-start.1
  28.4 0.0 copy-start.2
  28.4 0.0 copy-start.3
  28.5 1.7 %reshape.186.taps_ref = bf16[256,1152]{1,0:T(8,128)(2,1)} reshape(bf16[64,4,3,6,64]{4,3,2,1,0:T(8,128)(2,1)S(1)} %copy.17) | data formatting | bytes 1179648 | tf_op jit(solution)/shard_map/reshape | solution.py:202
  30.2 0.0 copy-done.1
  30.2 0.0 copy-done.2
  30.2 0.0 copy-done.3
  30.2 1.4 %broadcast_select_fusion = bf16[3,16,2,10,8,128]{5,4,3,2,1,0:T(8,128)(2,1)} fusion(pred[3,10,128]{2,1,0:T(8,128)(4,1)S(1)} %iota_compare_fusion, bf16[3,16,2,8,128]{4,3,2,1,0:T(8,128)(2,1)S(1)} %pad_maximum_fusion.1), kind=kLoop, calls=%fused_computation | loop fusion | flops 983040 | bytes 2166528 | tf_op jit(solution)/shard_map/jit(_where)/select_n | solution.py:195
  31.7 3.9 %all-to-all-done.inc_ref = bf16[384,8,128]{2,1,0:T(8,128)(2,1)S(1)} async-done(((bf16[384,8,128]{2,1,0:T(8,128)(2,1)}), bf16[384,8,128]{2,1,0:T(8,128)(2,1)S(1)}, u32[]{:S(2)}, u32[]{:S(2)}) %all-to-all-start) | async-done | bytes 786464 | tf_op jit(solution)/shard_map/all_to_all | solution.py:210
  35.5 0.0 copy-start
  35.5 0.9 %broadcast_in_dim.50.bias_ref = f32[256,128]{1,0:T(8,128)} broadcast(f32[256]{0:T(256)S(1)} %broadcast_in_dim.49), dimensions={0} | broadcast | bytes 132096 | tf_op jit(solution)/shard_map/broadcast_in_dim | solution.py:224
  36.4 0.0 copy-done
  36.5 23.2 %fine.1 = bf16[32,2,288,128]{3,2,1,0:T(8,128)(2,1)} custom-call(s32[200]{0:T(256)} %reshape.183.where_ref, bf16[384,8,128]{2,1,0:T(8,128)(2,1)} %copy-done, bf16[48,160,128]{2,1,0:T(8,128)(2,1)} %bitcast.29, bf16[256,1152]{1,0:T(8,128)(2,1)} %reshape.186.taps_ref, f32[256,128]{1,0:T(8,128)} %broadcast_in_dim.50.bias_ref, f32[18,128]{1,0:T(8,128)} %reshape.187.land_ref), custom_call_target="tpu_custom_call" | custom-call | tf_op jit(solution)/shard_map/fine/pallas_call | solution.py:166
  (6 shorter events, 0.1 us)
Async XLA Ops:
  7.2 14.5 %copy-start.6 = (bf16[16,256]{1,0:T(8,128)(2,1)S(1)}, bf16[16,256]{1,0:T(8,128)(2,1)}, u32[]{:S(2)}) copy-start(bf16[16,256]{1,0:T(8,128)(2,1)} %param.9) | copy-start | bytes 24580
  7.3 14.7 %copy-start.5 = (s32[128,144]{0,1:T(8,128)S(1)}, s32[128,144]{0,1:T(8,128)}, u32[]{:S(2)}) copy-start(s32[128,144]{0,1:T(8,128)} %param.13) | copy-start | bytes 221188
  7.3 28.3 %all-to-all-start = ((bf16[384,8,128]{2,1,0:T(8,128)(2,1)}), bf16[384,8,128]{2,1,0:T(8,128)(2,1)S(1)}, u32[]{:S(2)}, u32[]{:S(2)}) async-start(bf16[384,8,128]{2,1,0:T(8,128)(2,1)} %pack.1), calls=%async_computation | async-start | bytes 1572864 | tf_op jit(solution)/shard_map/all_to_all | solution.py:210
  23.0 1.7 %copy-start.4 = (bf16[3,3,64,64]{3,2,1,0:T(8,128)(2,1)S(1)}, bf16[3,3,64,64]{3,2,1,0:T(8,128)(2,1)}, u32[]{:S(2)}) copy-start(bf16[3,3,64,64]{3,2,1,0:T(8,128)(2,1)} %param.10) | copy-start | bytes 221188
  25.1 0.7 %copy-start.7 = (f32[64]{0:T(128)S(1)}, f32[64]{0:T(128)}, u32[]{:S(2)}) copy-start(f32[64]{0:T(128)} %param.11) | copy-start | bytes 772
  28.4 1.7 %copy-start.1 = (bf16[1,16,2,8,128]{4,3,2,1,0:T(8,128)(2,1)S(1)}, bf16[1,16,2,8,128]{4,3,2,1,0:T(8,128)(2,1)}, u32[]{:S(2)}) copy-start(bf16[1,16,2,8,128]{4,3,2,1,0:T(8,128)(2,1)} %get-tuple-element.9) | copy-start | bytes 196612
  28.4 1.7 %copy-start.2 = (bf16[1,16,2,8,128]{4,3,2,1,0:T(8,128)(2,1)S(1)}, bf16[1,16,2,8,128]{4,3,2,1,0:T(8,128)(2,1)}, u32[]{:S(2)}) copy-start(bf16[1,16,2,8,128]{4,3,2,1,0:T(8,128)(2,1)} %get-tuple-element.10) | copy-start | bytes 196612
  28.4 1.7 %copy-start.3 = (bf16[1,16,2,8,128]{4,3,2,1,0:T(8,128)(2,1)S(1)}, bf16[1,16,2,8,128]{4,3,2,1,0:T(8,128)(2,1)}, u32[]{:S(2)}) copy-start(bf16[1,16,2,8,128]{4,3,2,1,0:T(8,128)(2,1)} %get-tuple-element.11) | copy-start | bytes 196612
  35.5 0.9 %copy-start = (bf16[384,8,128]{2,1,0:T(8,128)(2,1)}, bf16[384,8,128]{2,1,0:T(8,128)(2,1)S(1)}, u32[]{:S(2)}) copy-start(bf16[384,8,128]{2,1,0:T(8,128)(2,1)S(1)} %all-to-all-done.inc_ref) | copy-start | bytes 2359300

commit v2 on v1

v2 whole, which is shorter than its diff:
```python
import jax
import jax.numpy as jnp
from jax import lax
from jax.experimental import pallas as pl
from jax.experimental.pallas import tpu as pltpu
from jax.sharding import PartitionSpec as P

PR = 18
PC = 8
CELLS = 16
WR = PR + 2
WC = PC + 2
MOST = 3
CB_ROWS = 24
CB_COLS = 40
HELD_ROWS = 20
C_IN = 69
C = 64
GRID_COLS = 640


def pack_body(ids_ref, coarse_ref, w_ref, out_ref, raw, weights, mixed, sems):
    n_lat, n_lon = 8, 16
    a = lax.axis_index("lat")
    b = lax.axis_index("lon")
    first = ids_ref[0, 0]
    owner = first // (CB_ROWS * CB_COLS)
    local = first % (CB_ROWS * CB_COLS)
    r0 = (local // CB_COLS) * n_lat + owner // n_lon
    c0 = (local % CB_COLS) * n_lon + owner % n_lon
    low = jnp.clip((r0 + 7) // 8 - 1, 0, CB_ROWS - HELD_ROWS)
    c_first = c0 - 1 + (b - c0 + 1 + 16 * CB_COLS) % n_lon
    lc_first = ((c_first + GRID_COLS) % GRID_COLS) // n_lon
    tile0 = lc_first // 8
    tile1 = (tile0 + 1) % (CB_COLS // 8)
    copies = []
    for slot, tile in ((0, tile0), (1, tile1)):
        copy = pltpu.make_async_copy(
            coarse_ref.at[pl.ds(low, HELD_ROWS), pl.ds(pl.multiple_of(tile * 8, 8), 8), :],
            raw.at[slot],
            sems.at[slot],
        )
        copy.start()
        copies.append(copy)
    w = w_ref[...].astype(jnp.float32).T
    weights[...] = jnp.zeros_like(weights)
    for j in range(8):
        weights[j, 10 * j : 10 * j + C_IN, 0:C] = w
        weights[j, 10 * j + C_IN : 10 * j + 2 * C_IN, C : 2 * C] = w
    for copy in copies:
        copy.wait()
    count = 2 * HELD_ROWS * 8
    for j in range(8):
        width = min(256, CELLS * C_IN - 128 * j)
        rows = raw[:, :, :, 128 * j : 128 * j + width].reshape(count, width)
        part = jnp.dot(
            rows, weights[j, 0:width, :].astype(jnp.bfloat16), preferred_element_type=jnp.float32
        )
        mixed[pl.ds(j, count, stride=8), :] = part
    starts = []
    for i in range(n_lat):
        top = r0 + PR * i - 1
        r_first = top + (a - top + 512) % n_lat
        lr = (r_first + 8) // 8 - 1 - low
        for m in range(MOST):
            starts.append(jnp.clip(lr + m, 0, HELD_ROWS - 1) * 8)

    def one_column(j, carry):
        left = c0 + PC * j - 1
        d = (b - left + 16 * CB_COLS) % n_lon
        n = (left + d - c_first) // n_lon
        pos = jnp.minimum(lc_first % 8 + n, 15)
        base = (pos // 8) * (HELD_ROWS * 8) + pos % 8
        for i in range(n_lat):
            for m in range(MOST):
                at = (base + starts[i * MOST + m]) * 8
                block = mixed[pl.ds(pl.multiple_of(at, 8), 8), :]
                out_ref[(i * n_lon + j) * MOST + m] = block.astype(jnp.bfloat16)
        return carry

    lax.fori_loop(0, n_lon, one_column, 0)


def pack(block_ids, coarse, w_mix):
    return pl.pallas_call(
        pack_body,
        out_shape=jax.ShapeDtypeStruct((128 * MOST, 8, 128), jnp.bfloat16),
        grid=(1,),
        in_specs=[
            pl.BlockSpec((8, 128), lambda g: (0, 0), memory_space=pltpu.SMEM),
            pl.BlockSpec(memory_space=pl.ANY),
            pl.BlockSpec((C, C_IN), lambda g: (0, 0)),
        ],
        out_specs=pl.BlockSpec((128 * MOST, 8, 128), lambda g: (0, 0, 0)),
        scratch_shapes=[
            pltpu.VMEM((2, HELD_ROWS, 8, CELLS * C_IN), jnp.bfloat16),
            pltpu.VMEM((8, 256, 2 * C), jnp.float32),
            pltpu.VMEM((2 * HELD_ROWS * 8 * 8, 128), jnp.float32),
            pltpu.SemaphoreType.DMA((2,)),
        ],
        name="pack",
    )(block_ids.T, coarse.reshape(CB_ROWS, CB_COLS, CELLS * C_IN), w_mix.T)


def fine_body(
    where_ref, bias_ref, land_ref, inc_hbm, spread_hbm, taps_hbm, out_hbm,
    inc, spread, taps, cells, cells_t, field, halo, bias, outs, in_sems, out_sems,
):
    loads = []
    for n, (source, target) in enumerate(((inc_hbm, inc), (spread_hbm, spread), (taps_hbm, taps))):
        load = pltpu.make_async_copy(source, target, in_sems.at[n])
        load.start()
        loads.append(load)
    for o in range(C):
        bias[o] = jnp.full((8, 128), bias_ref[o], jnp.float32)
    lower = lax.broadcasted_iota(jnp.int32, (8, 128), 1) < C
    loads[0].wait()
    for q in range(WR // 2):
        for col in range(WC):
            got = []
            for half in range(2):
                at = where_ref[(2 * q + half) * WC + col]
                block = inc[jnp.maximum(at, 0)].astype(jnp.float32)
                got.append(jnp.where(at >= 0, block, 0.0))
            u, v = got
            cells[q, 8 * col : 8 * col + 8, :] = jnp.where(lower, u, pltpu.roll(v, C, 1))
            cells[q, 8 * (WC + col) : 8 * (WC + col) + 8, :] = jnp.where(lower, pltpu.roll(u, C, 1), v)
    for q in range(WR // 2):
        cells_t[128 * q : 128 * q + 128, :] = cells[q].T.astype(jnp.bfloat16)
    loads[1].wait()

    def upsample(n, carry):
        right = jnp.concatenate([spread[4 * n + q] for q in range(4)], axis=1)
        fine = jnp.dot(
            cells_t[:, 0 : CELLS * WC], right, preferred_element_type=jnp.float32
        ).astype(jnp.bfloat16)
        for q in range(4):
            field[:, 4 * n + q] = fine[:, 128 * q : 128 * q + 128].reshape(WR, C, 128)
        return carry

    lax.fori_loop(0, 4, upsample, 0)
    edge = jnp.dot(cells_t[:, 0 : CELLS * WC], spread[16], preferred_element_type=jnp.float32)
    halo[...] = edge.astype(jnp.bfloat16).reshape(WR, C, 128)
    loads[2].wait()
    lane = lax.broadcasted_iota(jnp.int32, (C, 128), 1)
    spot = lax.broadcasted_iota(jnp.int32, (16, 8, 128), 1) // 2

    def band(step):
        centre = []
        left = []
        right = []
        for rr in range(18):
            row = 15 + rr
            mid = field[step + row // 16, row % 16]
            side = pltpu.roll(halo[step + row // 16], 127 - 2 * (row % 16), 1)
            centre.append(mid)
            left.append(jnp.where(lane == 0, side, pltpu.roll(mid, 1, 1)))
            right.append(jnp.where(lane == 127, side, pltpu.roll(mid, 127, 1)))
        totals = []
        for k in range(4):
            columns = []
            for hb in range(2):
                at = 2 * (4 * hb + k)
                columns.append(
                    jnp.concatenate(left[at : at + 4] + centre[at : at + 4] + right[at : at + 4], axis=0)
                )
            totals.append(
                jnp.dot(taps[k], jnp.concatenate(columns, axis=1), preferred_element_type=jnp.float32)
            )
        land = land_ref[pl.ds(step, 1), :]
        for u in range(4):
            halves = []
            for hb in range(2):
                t = [total[:, 128 * hb : 128 * hb + 128].reshape(16, 8, 128) for total in totals]
                got = t[3]
                for k in range(3):
                    got = jnp.where(spot == (u + k) % 4, t[k], got)
                if u > 0:
                    got = pltpu.roll(got, 8 - 2 * u, 1)
                halves.append((got + bias[16 * u : 16 * u + 16]) * land)
            outs[step, :, u] = jnp.concatenate(halves, axis=1).astype(jnp.bfloat16)

    def store(step):
        rows = pl.ds(step * 16 if isinstance(step, int) else pl.multiple_of(step * 16, 16), 16)
        return pltpu.make_async_copy(outs.at[step], out_hbm.at[:, :, rows, :], out_sems.at[step])

    def two_bands(t, carry):
        for half in range(2):
            step = 2 * t + half
            band(step)
            store(step).start()
        return carry

    lax.fori_loop(0, PR // 2, two_bands, 0)
    for step in range(PR):
        store(step).wait()


def fine(where, bias_order, land, incoming, spread, taps):
    return pl.pallas_call(
        fine_body,
        out_shape=jax.ShapeDtypeStruct((C // 4, 4, PR * 16, 128), jnp.bfloat16),
        in_specs=[
            pl.BlockSpec(memory_space=pltpu.SMEM),
            pl.BlockSpec(memory_space=pltpu.SMEM),
            pl.BlockSpec(memory_space=pltpu.VMEM),
            pl.BlockSpec(memory_space=pl.ANY),
            pl.BlockSpec(memory_space=pl.ANY),
            pl.BlockSpec(memory_space=pl.ANY),
        ],
        out_specs=pl.BlockSpec(memory_space=pl.ANY),
        scratch_shapes=[
            pltpu.VMEM((128 * MOST, 8, 128), jnp.bfloat16),
            pltpu.VMEM((17, CELLS * WC, 128), jnp.bfloat16),
            pltpu.VMEM((4, 2 * C, 12 * C), jnp.bfloat16),
            pltpu.VMEM((WR // 2, 256, 128), jnp.float32),
            pltpu.VMEM((WR * C, 256), jnp.bfloat16),
            pltpu.VMEM((WR, 16, C, 128), jnp.bfloat16),
            pltpu.VMEM((WR, C, 128), jnp.bfloat16),
            pltpu.VMEM((C, 8, 128), jnp.float32),
            pltpu.VMEM((PR, C // 4, 4, 16, 128), jnp.bfloat16),
            pltpu.SemaphoreType.DMA((3,)),
            pltpu.SemaphoreType.DMA((PR,)),
        ],
        name="fine",
    )(where, bias_order, land, incoming, spread, taps)


def spread_of(interp):
    cells = interp.reshape(8, 2, 16, 16).transpose(2, 1, 0, 3)
    wide = jnp.tile(cells, (1, 1, 1, PC))
    same = jnp.arange(128)[None, :] // 16 + 1 == jnp.arange(WC)[:, None]
    inner = jnp.where(same[None, None, :, None, :], wide[:, :, None], 0)
    edges = jnp.stack([cells[..., 0], cells[..., 15]], axis=1).reshape(32, 2, 8).transpose(1, 2, 0)
    edges = jnp.pad(edges, ((0, 0), (0, 0), (0, 96)))
    column = jnp.where(jnp.arange(128) % 2 == 0, WC - 1, 0)
    same = column[None, :] == jnp.arange(WC)[:, None]
    outer = jnp.where(same[None, :, None, :], edges[:, None], 0)
    full = jnp.concatenate([inner, outer[None]], axis=0)
    return full.reshape(17, CELLS * WC, 128).astype(jnp.bfloat16)


def taps_of(kernel):
    by = kernel.transpose(2, 1, 0, 3)
    rows = jnp.stack([jnp.pad(by, ((0, 0), (0, 0), (r, 1 - r), (0, 0))) for r in range(2)], axis=1)
    rows = rows.reshape(C // 4, 4, 2, 12 * C)
    return jnp.stack([jnp.roll(rows, k, axis=1) for k in range(4)]).reshape(4, 2 * C, 12 * C)


def per_device(coarse, w_mix, interp, kernel, bias, block_ids, valid):
    n_lat, n_lon = 8, 16
    i = lax.axis_index("lat")
    j = lax.axis_index("lon")
    outgoing = pack(block_ids, coarse, w_mix)
    incoming = lax.all_to_all(outgoing, ("lat", "lon"), split_axis=0, concat_axis=0, tiled=True)
    first = block_ids[0, 0]
    owner = first // (CB_ROWS * CB_COLS)
    local = first % (CB_ROWS * CB_COLS)
    r0 = (local // CB_COLS) * n_lat + owner // n_lon
    c0 = (local % CB_COLS) * n_lon + owner % n_lon
    grid = valid.reshape(n_lat, n_lon, PR, PC).transpose(0, 2, 1, 3).reshape(n_lat * PR, n_lon * PC)
    window = lax.dynamic_slice(jnp.pad(grid, 1), (i * PR, j * PC), (WR, WC))
    row = jnp.arange(WR)[:, None]
    col = jnp.arange(WC)[None, :]
    source = (r0 + PR * i - 1 + row + 8) % n_lat * n_lon + (c0 + PC * j - 1 + col + 16) % n_lon
    where = jnp.where(window > 0, source * MOST + row // 8, -1).reshape(WR * WC).astype(jnp.int32)
    own = window[1:-1, 1:-1].astype(jnp.float32)
    land = jnp.repeat(own, 16, axis=1)
    bias_order = bias.reshape(C // 4, 4).T.reshape(C)
    out = fine(where, bias_order, land, incoming, spread_of(interp), taps_of(kernel))
    return out.reshape(C, PR * 16, 128)


def solution(mesh):
    placed = (P(("lat", "lon"), None), P(), P(), P(), P(), P(), P())
    return jax.shard_map(
        per_device, mesh=mesh, in_specs=placed, out_specs=P(None, "lat", "lon"), check_vma=False
    )
```

time: 60.1 us -> 48.1 us (0.80)
  Pallas kernels: 27.4 us -> 18.6 us
  local copies, waits for them, and re-layouts: 13 us -> 9.37 us
  other arithmetic: 1.99 us -> 3.01 us
  waiting for transfers between devices: 3.86 us -> 2.91 us
    pallas_call x1, Pallas kernels: 23.2 us -> 14.3 us  [fine(): pl.pallas_call(fine_body, out_shape=jax.ShapeDtypeStruct((C // 4, 4, PR *...]
    unnamed x18 -> x13, local copies, waits for them, and re-layouts: 3.36 us -> 1.16 us
    concatenate x0 -> x3, other arithmetic: none -> 1.54 us  [the longest x1 0.92 us: spread_of(): full = jnp.concatenate([inner, outer[None]], axis=0)]
    select_n x2 -> x3, other arithmetic: 1.43 us -> 0.06 us  [the longest x1 0.05 us: spread_of(): inner = jnp.where(same[None, None, :, None, :], wide[:, :, None], 0)]
    another operation x5 -> x13, local copies, waits for them, and re-layouts: 2.77 us -> 1.68 us  [the longest x6 0.82 us: taps_of(): jnp.stack([jnp.pad(by, ((0, 0), (0, 0), (r, 1 - r), (0, 0))) for r in ran...]
    broadcast_in_dim x3 -> x1, local copies, waits for them, and re-layouts: 1.08 us -> 0.01 us  [spread_of(): inner = jnp.where(same[None, None, :, None, :], wide[:, :, None], 0)]
    reshape x1 -> x2, local copies, waits for them, and re-layouts: 1.71 us -> 0.71 us  [per_device(): bias_order = bias.reshape(C // 4, 4).T.reshape(C)]
    all_to_all x1, waiting for transfers between devices: 3.86 us -> 2.91 us  [per_device(): lax.all_to_all(outgoing, ('lat', 'lon'), split_axis=0, concat_axis=0, til...]
  transfers between devices with their start and end apart: 1 -> 1, of which waited for: 1 -> 1; matrix products, arithmetic and copies ran while one was open for 18% -> 24% of each run, Pallas kernels for 0% -> 0%
where the time goes in v2:
time: 48.1 us; the launch traced here: 47.7 us
  Pallas kernels  18.6 us (39%)
  starting transfers between devices  11.5 us (24%)
  local copies, waits for them, and re-layouts  9.37 us (19%)
  other arithmetic  3.01 us (6%)
  waiting for transfers between devices  2.91 us (6%)
  between operations  2.39 us (5%)
    pallas_call x1, Pallas kernels, fine(): pl.pallas_call(fine_body, out_shape=jax.ShapeDtypeStruct((C // 4, 4, PR *...  14.3 us
    all_to_all x1, starting transfers between devices, per_device(): lax.all_to_all(outgoing, ('lat', 'lon'), split_axis=0, concat_axis=0, til...  11.5 us
    pallas_call x1, Pallas kernels, pack(): pl.pallas_call(pack_body, out_shape=jax.ShapeDtypeStruct((128 * MOST, 8,...  4.3 us
    all_to_all x1, waiting for transfers between devices, per_device(): lax.all_to_all(outgoing, ('lat', 'lon'), split_axis=0, concat_axis=0, til...  2.91 us
    slice x1, local copies, waits for them, and re-layouts, per_device(): first = block_ids[0, 0]  1.23 us
    unnamed x13, local copies, waits for them, and re-layouts  1.16 us
    another operation x1, other arithmetic, taps_of(): jnp.stack([jnp.roll(rows, k, axis=1) for k in range(4)])  1.02 us
  transfers between devices with their start and end apart: 1, of which 1 were waited for; matrix products, arithmetic and copies ran while one was open for 24% of the time, Pallas kernels for 0%

profile of v2, /device:TPU:1, one launch (start us, length us, event | category | flops | bytes accessed | tf_op | source)
XLA Modules:
  0.0 47.7 jit_solution(6861465835657848664)
XLA Ops:
  0.0 4.3 %pack.1 = bf16[384,8,128]{2,1,0:T(8,128)(2,1)} custom-call(s32[144,128]{1,0:T(8,128)} %bitcast.35, bf16[24,40,1104]{2,1,0:T(8,128)(2,1)} %bitcast.29, bf16[64,69]{1,0:T(8,128)(2,1)} %bitcast.38), custom_call_target="tpu_custom_call" | custom-call | tf_op jit(solution)/shard_map/pack/pallas_call | solution.py:85
  4.3 11.5 %all-to-all-start = ((bf16[384,8,128]{2,1,0:T(8,128)(2,1)}), bf16[384,8,128]{2,1,0:T(8,128)(2,1)S(1)}, u32[]{:S(2)}, u32[]{:S(2)}) async-start(bf16[384,8,128]{2,1,0:T(8,128)(2,1)} %pack.1), calls=%async_computation | async-start | bytes 1572864 | tf_op jit(solution)/shard_map/all_to_all | solution.py:255
  15.8 1.2 %slice.36 = s32[1,1]{0,1:T(1,128)} slice(s32[128,144]{0,1:T(8,128)} %param.12), slice={[0:1], [0:1]} | slice | bytes 8 | tf_op jit(solution)/shard_map/slice | solution.py:256
  19.0 0.1 reshape.274
  19.2 0.1 fusion.10
  19.3 0.1 copy.61
  19.4 0.2 fusion.9
  19.7 0.1 stack.39
  19.8 0.1 stack.35
  20.0 0.1 stack.38
  20.1 0.1 stack.34
  20.4 0.1 fusion.8
  20.5 0.1 fusion.6
  20.7 0.1 fusion.7
  20.9 0.1 reshape.270
  21.0 0.1 copy.45
  21.1 0.6 %reshape.271.bias_ref = f32[64]{0:T(128)} reshape(f32[4,16]{1,0:T(4,128)S(1)} %copy.45) | data formatting | bytes 512 | tf_op jit(solution)/shard_map/reshape | solution.py:269
  21.7 0.2 copy.48
  21.9 0.2 copy.49
  22.1 0.1 copy.50
  22.2 0.1 copy.60
  22.3 0.1 pad_maximum_fusion.2
  22.4 0.2 copy.54
  22.6 0.1 stack.37
  22.7 0.2 pad_maximum_fusion.4
  22.9 0.2 copy.58
  23.2 0.1 stack.42
  23.2 0.4 pad_maximum_fusion.3
  23.7 0.2 copy.57
  23.9 0.1 stack.41
  24.0 0.2 copy.59
  24.2 0.1 stack.43
  24.3 0.1 tile.8
  24.4 0.3 tile.9
  24.7 0.2 reshape.267
  24.9 0.7 %copy.43 = s32[8,18,16,8]{1,0,3,2:T(8,128)S(1)} copy(s32[8,18,16,8]{2,0,3,1:T(8,128)S(1)} %bitcast.28) | data formatting | bytes 147456 | tf_op jit(solution)/shard_map/transpose | solution.py:261
  25.6 0.2 reshape.268
  25.8 0.1 add_select_fusion
  25.9 0.1 copy.44
  26.0 0.6 %reshape.269.where_ref = s32[200]{0:T(256)} reshape(s32[20,10]{1,0:T(8,128)S(1)} %copy.44) | data formatting | bytes 1600 | tf_op jit(solution)/shard_map/reshape | solution.py:266
  26.7 0.1 fusion.1
  26.7 0.1 copy.46
  26.9 0.7 %reshape.272.land_ref = f32[18,128]{1,0:T(8,128)} reshape(f32[18,8,16]{2,1,0:T(8,128)S(1)} %broadcast_in_dim.70) | data formatting | bytes 18432 | tf_op jit(solution)/shard_map/reshape | solution.py:268
  27.7 0.9 %pad_maximum_fusion.1.spread_hbm = bf16[17,160,128]{2,1,0:T(8,128)(2,1)} fusion(bf16[1,160,128]{2,1,0:T(8,128)(2,1)S(1)} %bitcast.32, bf16[16,160,128]{2,1,0:T(8,128)(2,1)S(1)} %bitcast_select_fusion), kind=kLoop, calls=%fused_computation.1 | loop fusion | flops 348160 | bytes 1392640 | tf_op jit(solution)/shard_map/concatenate | solution.py:239
  28.6 1.0 %pad_maximum_fusion.taps_hbm = bf16[4,128,768]{2,1,0:T(8,128)(2,1)} fusion(bf16[1,128,768]{2,1,0:T(8,128)(2,1)S(1)} %stack.43, bf16[1,128,768]{2,1,0:T(8,128)(2,1)S(1)} %stack.42, bf16[1,128,768]{2,1,0:T(8,128)(2,1)S(1)} %stack.41, bf16[1,128,768]{2,1,0:T(8,128)(2,1)S(1)} %stack.37), kind=kLoop, calls=%fused_computation | loop fusion | flops 1179648 | bytes 1572864 | tf_op jit(solution)/shard_map/stack | solution.py:247
  29.7 2.9 %all-to-all-done.inc_hbm = bf16[384,8,128]{2,1,0:T(8,128)(2,1)S(1)} async-done(((bf16[384,8,128]{2,1,0:T(8,128)(2,1)}), bf16[384,8,128]{2,1,0:T(8,128)(2,1)S(1)}, u32[]{:S(2)}, u32[]{:S(2)}) %all-to-all-start) | async-done | bytes 786464 | tf_op jit(solution)/shard_map/all_to_all | solution.py:255
  32.6 0.9 %copy-done = bf16[384,8,128]{2,1,0:T(8,128)(2,1)} copy-done((bf16[384,8,128]{2,1,0:T(8,128)(2,1)}, bf16[384,8,128]{2,1,0:T(8,128)(2,1)S(1)}, u32[]{:S(2)}) %copy-start) | copy-done | bytes 786456
  33.5 14.3 %fine.1 = bf16[16,4,288,128]{3,2,1,0:T(8,128)(2,1)} custom-call(s32[200]{0:T(256)} %reshape.269.where_ref, f32[64]{0:T(128)} %reshape.271.bias_ref, f32[18,128]{1,0:T(8,128)} %reshape.272.land_ref, bf16[384,8,128]{2,1,0:T(8,128)(2,1)} %copy-done, bf16[17,160,128]{2,1,0:T(8,128)(2,1)} %pad_maximum_fusion.1.spread_hbm, ...), custom_call_target="tpu_custom_call" | custom-call | tf_op jit(solution)/shard_map/fine/pallas_call | solution.py:200
  (24 shorter events, 0.3 us)
Async XLA Ops:
  0.0 19.0 %copy-start.3 = (bf16[16,256]{1,0:T(8,128)(2,1)S(1)}, bf16[16,256]{1,0:T(8,128)(2,1)}, u32[]{:S(2)}) copy-start(bf16[16,256]{1,0:T(8,128)(2,1)} %param.9) | copy-start | bytes 24580
  0.0 19.3 %copy-start.1 = (bf16[3,3,64,64]{3,2,1,0:T(8,128)(2,1)S(1)}, bf16[3,3,64,64]{3,2,1,0:T(8,128)(2,1)}, u32[]{:S(2)}) copy-start(bf16[3,3,64,64]{3,2,1,0:T(8,128)(2,1)} %param.10) | copy-start | bytes 221188
  0.0 20.9 %copy-start.4 = (f32[64]{0:T(128)S(1)}, f32[64]{0:T(128)}, u32[]{:S(2)}) copy-start(f32[64]{0:T(128)} %param.11) | copy-start | bytes 772
  4.3 28.3 %all-to-all-start = ((bf16[384,8,128]{2,1,0:T(8,128)(2,1)}), bf16[384,8,128]{2,1,0:T(8,128)(2,1)S(1)}, u32[]{:S(2)}, u32[]{:S(2)}) async-start(bf16[384,8,128]{2,1,0:T(8,128)(2,1)} %pack.1), calls=%async_computation | async-start | bytes 1572864 | tf_op jit(solution)/shard_map/all_to_all | solution.py:255
  19.7 5.1 %copy-start.2 = (s32[128,144]{0,1:T(8,128)S(1)}, s32[128,144]{0,1:T(8,128)}, u32[]{:S(2)}) copy-start(s32[128,144]{0,1:T(8,128)} %param.13) | copy-start | bytes 221188
  32.6 0.9 %copy-start = (bf16[384,8,128]{2,1,0:T(8,128)(2,1)}, bf16[384,8,128]{2,1,0:T(8,128)(2,1)S(1)}, u32[]{:S(2)}) copy-start(bf16[384,8,128]{2,1,0:T(8,128)(2,1)S(1)} %all-to-all-done.inc_hbm) | copy-start | bytes 2359300

commit v3 on v2

--- a/solution.py
+++ b/solution.py
@@ -63,58 +63,48 @@
         r_first = top + (a - top + 512) % n_lat
         lr = (r_first + 8) // 8 - 1 - low
         for m in range(MOST):
-            starts.append(jnp.clip(lr + m, 0, HELD_ROWS - 1) * 8)
-
-    def one_column(j, carry):
+            starts.append(jnp.clip(lr + m, 0, HELD_ROWS - 1) * 64)
+    for j in range(n_lon):
         left = c0 + PC * j - 1
         d = (b - left + 16 * CB_COLS) % n_lon
         n = (left + d - c_first) // n_lon
         pos = jnp.minimum(lc_first % 8 + n, 15)
-        base = (pos // 8) * (HELD_ROWS * 8) + pos % 8
+        base = ((pos // 8) * (HELD_ROWS * 8) + pos % 8) * 8
         for i in range(n_lat):
             for m in range(MOST):
-                at = (base + starts[i * MOST + m]) * 8
-                block = mixed[pl.ds(pl.multiple_of(at, 8), 8), :]
+                block = mixed[pl.ds(pl.multiple_of(base + starts[i * MOST + m], 8), 8), :]
                 out_ref[(i * n_lon + j) * MOST + m] = block.astype(jnp.bfloat16)
-        return carry
-
-    lax.fori_loop(0, n_lon, one_column, 0)
 
 
 def pack(block_ids, coarse, w_mix):
     return pl.pallas_call(
         pack_body,
-        out_shape=jax.ShapeDtypeStruct((128 * MOST, 8, 128), jnp.bfloat16),
+        out_shape=pltpu.VMEM((128 * MOST, 8, 128), jnp.bfloat16),
         grid=(1,),
         in_specs=[
             pl.BlockSpec((8, 128), lambda g: (0, 0), memory_space=pltpu.SMEM),
             pl.BlockSpec(memory_space=pl.ANY),
             pl.BlockSpec((C, C_IN), lambda g: (0, 0)),
         ],
-        out_specs=pl.BlockSpec((128 * MOST, 8, 128), lambda g: (0, 0, 0)),
+        out_specs=pl.BlockSpec(memory_space=pltpu.VMEM),
         scratch_shapes=[
             pltpu.VMEM((2, HELD_ROWS, 8, CELLS * C_IN), jnp.bfloat16),
             pltpu.VMEM((8, 256, 2 * C), jnp.float32),
             pltpu.VMEM((2 * HELD_ROWS * 8 * 8, 128), jnp.float32),
             pltpu.SemaphoreType.DMA((2,)),
         ],
+        compiler_params=pltpu.CompilerParams(vmem_limit_bytes=40 << 20),
         name="pack",
-    )(block_ids.T, coarse.reshape(CB_ROWS, CB_COLS, CELLS * C_IN), w_mix.T)
+    )(block_ids, coarse, w_mix)
 
 
 def fine_body(
-    where_ref, bias_ref, land_ref, inc_hbm, spread_hbm, taps_hbm, out_hbm,
-    inc, spread, taps, cells, cells_t, field, halo, bias, outs, in_sems, out_sems,
+    where_ref, bias_ref, land_ref, inc, spread, taps, out_hbm,
+    cells, cells_t, field, halo, bias, outs, out_sems,
 ):
-    loads = []
-    for n, (source, target) in enumerate(((inc_hbm, inc), (spread_hbm, spread), (taps_hbm, taps))):
-        load = pltpu.make_async_copy(source, target, in_sems.at[n])
-        load.start()
-        loads.append(load)
     for o in range(C):
         bias[o] = jnp.full((8, 128), bias_ref[o], jnp.float32)
     lower = lax.broadcasted_iota(jnp.int32, (8, 128), 1) < C
-    loads[0].wait()
     for q in range(WR // 2):
         for col in range(WC):
             got = []
@@ -127,47 +117,41 @@
             cells[q, 8 * (WC + col) : 8 * (WC + col) + 8, :] = jnp.where(lower, pltpu.roll(u, C, 1), v)
     for q in range(WR // 2):
         cells_t[128 * q : 128 * q + 128, :] = cells[q].T.astype(jnp.bfloat16)
-    loads[1].wait()
-
-    def upsample(n, carry):
-        right = jnp.concatenate([spread[4 * n + q] for q in range(4)], axis=1)
+
+    edge = jnp.dot(cells_t[:, 0 : CELLS * WC], spread[16], preferred_element_type=jnp.float32)
+    halo[...] = edge.astype(jnp.bfloat16)
+    lane = lax.broadcasted_iota(jnp.int32, (WR * C, 128), 1)
+    for n in range(4):
+        wide = jnp.concatenate([spread[4 * n + q] for q in range(4)], axis=1)
         fine = jnp.dot(
-            cells_t[:, 0 : CELLS * WC], right, preferred_element_type=jnp.float32
+            cells_t[:, 0 : CELLS * WC], wide, preferred_element_type=jnp.float32
         ).astype(jnp.bfloat16)
         for q in range(4):
-            field[:, 4 * n + q] = fine[:, 128 * q : 128 * q + 128].reshape(WR, C, 128)
-        return carry
-
-    lax.fori_loop(0, 4, upsample, 0)
-    edge = jnp.dot(cells_t[:, 0 : CELLS * WC], spread[16], preferred_element_type=jnp.float32)
-    halo[...] = edge.astype(jnp.bfloat16).reshape(WR, C, 128)
-    loads[2].wait()
-    lane = lax.broadcasted_iota(jnp.int32, (C, 128), 1)
+            row = 4 * n + q
+            mid = fine[:, 128 * q : 128 * q + 128]
+            side = pltpu.roll(halo[...], 127 - 2 * row, 1)
+            left = jnp.where(lane == 0, side, pltpu.roll(mid, 1, 1))
+            right = jnp.where(lane == 127, side, pltpu.roll(mid, 127, 1))
+            for tap, part in enumerate((left, mid, right)):
+                field[tap, :, row] = part.reshape(WR, C, 128)
     spot = lax.broadcasted_iota(jnp.int32, (16, 8, 128), 1) // 2
 
     def band(step):
-        centre = []
-        left = []
-        right = []
-        for rr in range(18):
-            row = 15 + rr
-            mid = field[step + row // 16, row % 16]
-            side = pltpu.roll(halo[step + row // 16], 127 - 2 * (row % 16), 1)
-            centre.append(mid)
-            left.append(jnp.where(lane == 0, side, pltpu.roll(mid, 1, 1)))
-            right.append(jnp.where(lane == 127, side, pltpu.roll(mid, 127, 1)))
         totals = []
         for k in range(4):
             columns = []
             for hb in range(2):
                 at = 2 * (4 * hb + k)
-                columns.append(
-                    jnp.concatenate(left[at : at + 4] + centre[at : at + 4] + right[at : at + 4], axis=0)
-                )
+                parts = []
+                for tap in range(3):
+                    for rr in range(at, at + 4):
+                        row = 15 + rr
+                        parts.append(field[tap, step + row // 16, row % 16])
+                columns.append(jnp.concatenate(parts, axis=0))
             totals.append(
                 jnp.dot(taps[k], jnp.concatenate(columns, axis=1), preferred_element_type=jnp.float32)
             )
-        land = land_ref[pl.ds(step, 1), :]
+        land = land_ref[step : step + 1, :]
         for u in range(4):
             halves = []
             for hb in range(2):
@@ -181,17 +165,13 @@
             outs[step, :, u] = jnp.concatenate(halves, axis=1).astype(jnp.bfloat16)
 
     def store(step):
-        rows = pl.ds(step * 16 if isinstance(step, int) else pl.multiple_of(step * 16, 16), 16)
-        return pltpu.make_async_copy(outs.at[step], out_hbm.at[:, :, rows, :], out_sems.at[step])
-
-    def two_bands(t, carry):
-        for half in range(2):
-            step = 2 * t + half
-            band(step)
-            store(step).start()
-        return carry
-
-    lax.fori_loop(0, PR // 2, two_bands, 0)
+        return pltpu.make_async_copy(
+            outs.at[step], out_hbm.at[:, :, step * 16 : step * 16 + 16, :], out_sems.at[step]
+        )
+
+    for step in range(PR):
+        band(step)
+        store(step).start()
     for step in range(PR):
         store(step).wait()
 
@@ -204,24 +184,21 @@
             pl.BlockSpec(memory_space=pltpu.SMEM),
             pl.BlockSpec(memory_space=pltpu.SMEM),
             pl.BlockSpec(memory_space=pltpu.VMEM),
-            pl.BlockSpec(memory_space=pl.ANY),
-            pl.BlockSpec(memory_space=pl.ANY),
-            pl.BlockSpec(memory_space=pl.ANY),
+            pl.BlockSpec(memory_space=pltpu.VMEM),
+            pl.BlockSpec(memory_space=pltpu.VMEM),
+            pl.BlockSpec(memory_space=pltpu.VMEM),
         ],
         out_specs=pl.BlockSpec(memory_space=pl.ANY),
         scratch_shapes=[
-            pltpu.VMEM((128 * MOST, 8, 128), jnp.bfloat16),
-            pltpu.VMEM((17, CELLS * WC, 128), jnp.bfloat16),
-            pltpu.VMEM((4, 2 * C, 12 * C), jnp.bfloat16),
             pltpu.VMEM((WR // 2, 256, 128), jnp.float32),
             pltpu.VMEM((WR * C, 256), jnp.bfloat16),
-            pltpu.VMEM((WR, 16, C, 128), jnp.bfloat16),
-            pltpu.VMEM((WR, C, 128), jnp.bfloat16),
+            pltpu.VMEM((3, WR, 16, C, 128), jnp.bfloat16),
+            pltpu.VMEM((WR * C, 128), jnp.bfloat16),
             pltpu.VMEM((C, 8, 128), jnp.float32),
             pltpu.VMEM((PR, C // 4, 4, 16, 128), jnp.bfloat16),
-            pltpu.SemaphoreType.DMA((3,)),
             pltpu.SemaphoreType.DMA((PR,)),
         ],
+        compiler_params=pltpu.CompilerParams(vmem_limit_bytes=40 << 20),
         name="fine",
     )(where, bias_order, land, incoming, spread, taps)
 
@@ -251,7 +228,8 @@
     n_lat, n_lon = 8, 16
     i = lax.axis_index("lat")
     j = lax.axis_index("lon")
-    outgoing = pack(block_ids, coarse, w_mix)
+    far = (pltpu.with_memory_space_constraint(v, pltpu.HBM) for v in (block_ids.T, coarse.reshape(CB_ROWS, CB_COLS, CELLS * C_IN), w_mix.T))
+    outgoing = pack(*far)
     incoming = lax.all_to_all(outgoing, ("lat", "lon"), split_axis=0, concat_axis=0, tiled=True)
     first = block_ids[0, 0]
     owner = first // (CB_ROWS * CB_COLS)
@@ -267,7 +245,9 @@
     own = window[1:-1, 1:-1].astype(jnp.float32)
     land = jnp.repeat(own, 16, axis=1)
     bias_order = bias.reshape(C // 4, 4).T.reshape(C)
-    out = fine(where, bias_order, land, incoming, spread_of(interp), taps_of(kernel))
+    near = (land, incoming, spread_of(interp), taps_of(kernel))
+    near = tuple(pltpu.with_memory_space_constraint(v, pltpu.VMEM) for v in near)
+    out = fine(where, bias_order, *near)
     return out.reshape(C, PR * 16, 128)
 
 

time: 48.1 us -> 41 us (0.85)
  Pallas kernels: 18.6 us -> 12.4 us
  waiting for transfers between devices: 2.91 us -> 6.55 us
  local copies, waits for them, and re-layouts: 9.37 us -> 6.76 us
  other arithmetic: 3.01 us -> 1.25 us
    pallas_call x1, Pallas kernels: 14.3 us -> 8.54 us  [fine(): pl.pallas_call(fine_body, out_shape=jax.ShapeDtypeStruct((C // 4, 4, PR *...]
    all_to_all x1, waiting for transfers between devices: 2.91 us -> 6.55 us  [per_device(): lax.all_to_all(outgoing, ('lat', 'lon'), split_axis=0, concat_axis=0, til...]
    another operation x1, other arithmetic: 1.02 us -> 0.1 us  [taps_of(): jnp.stack([jnp.roll(rows, k, axis=1) for k in range(4)])]
    unnamed x13 -> x11, local copies, waits for them, and re-layouts: 1.16 us -> 0.26 us
    concatenate x1, other arithmetic: 0.92 us -> 0.06 us  [spread_of(): full = jnp.concatenate([inner, outer[None]], axis=0)]
    reshape x1, local copies, waits for them, and re-layouts: 0.7 us -> 0.09 us  [per_device(): land = jnp.repeat(own, 16, axis=1)]
    reshape x2, local copies, waits for them, and re-layouts: 0.71 us -> 0.16 us  [per_device(): bias_order = bias.reshape(C // 4, 4).T.reshape(C)]
    reshape x1, local copies, waits for them, and re-layouts: 0.63 us -> 0.09 us  [per_device(): jnp.where(window > 0, source * MOST + row // 8, -1).reshape(WR * WC)]
  transfers between devices with their start and end apart: 1 -> 1, of which waited for: 1 -> 1; matrix products, arithmetic and copies ran while one was open for 24% -> 20% of each run, Pallas kernels for 0% -> 0%
where the time goes in v3:
time: 41 us; the launch traced here: 40.7 us
  Pallas kernels  12.4 us (30%)
  starting transfers between devices  11.5 us (28%)
  local copies, waits for them, and re-layouts  6.76 us (16%)
  waiting for transfers between devices  6.55 us (16%)
  between operations  2.22 us (5%)
  other arithmetic  1.25 us (3%)
    all_to_all x1, starting transfers between devices, per_device(): lax.all_to_all(outgoing, ('lat', 'lon'), split_axis=0, concat_axis=0, til...  11.5 us
    pallas_call x1, Pallas kernels, fine(): pl.pallas_call(fine_body, out_shape=jax.ShapeDtypeStruct((C // 4, 4, PR *...  8.54 us
    all_to_all x1, waiting for transfers between devices, per_device(): lax.all_to_all(outgoing, ('lat', 'lon'), split_axis=0, concat_axis=0, til...  6.55 us
    pallas_call x1, Pallas kernels, pack(): pl.pallas_call(pack_body, out_shape=pltpu.VMEM((128 * MOST, 8, 128), jnp....  3.9 us
    slice x1, local copies, waits for them, and re-layouts, per_device(): first = block_ids[0, 0]  1.2 us
    another operation x6, local copies, waits for them, and re-layouts, taps_of(): jnp.stack([jnp.pad(by, ((0, 0), (0, 0), (r, 1 - r), (0, 0))) for r in ran...  0.82 us
  transfers between devices with their start and end apart: 1, of which 1 were waited for; matrix products, arithmetic and copies ran while one was open for 20% of the time, Pallas kernels for 0%

profile of v3, /device:TPU:1, one launch (start us, length us, event | category | flops | bytes accessed | tf_op | source)
XLA Modules:
  0.0 40.7 jit_solution(1068656068605305297)
XLA Ops:
  0.0 3.9 %pack.1 = bf16[384,8,128]{2,1,0:T(8,128)(2,1)} custom-call(s32[144,128]{1,0:T(8,128)} %bitcast.35, bf16[24,40,1104]{2,1,0:T(8,128)(2,1)} %bitcast.29, bf16[64,69]{1,0:T(8,128)(2,1)} %bitcast.38), custom_call_target="tpu_custom_call" | custom-call | tf_op jit(solution)/shard_map/pack/pallas_call | solution.py:80
  3.9 11.5 %all-to-all-start = ((bf16[384,8,128]{2,1,0:T(8,128)(2,1)}), bf16[384,8,128]{2,1,0:T(8,128)(2,1)S(1)}, u32[]{:S(2)}, u32[]{:S(2)}) async-start(bf16[384,8,128]{2,1,0:T(8,128)(2,1)} %pack.1), calls=%async_computation | async-start | bytes 1572864 | tf_op jit(solution)/shard_map/all_to_all | solution.py:233
  15.4 1.2 %slice.36 = s32[1,1]{0,1:T(1,128)} slice(s32[128,144]{0,1:T(8,128)} %param.12), slice={[0:1], [0:1]} | slice | bytes 8 | tf_op jit(solution)/shard_map/slice | solution.py:234
  18.4 0.1 reshape.274
  18.5 0.1 fusion.10
  18.6 0.1 copy.61
  18.8 0.2 fusion.9
  19.0 0.1 stack.39
  19.2 0.1 stack.35
  19.3 0.1 stack.38
  19.5 0.1 stack.34
  19.7 0.1 fusion.8
  19.9 0.1 fusion.6
  20.0 0.1 fusion.7
  20.3 0.1 reshape.270
  20.4 0.1 copy.45
  20.5 0.1 reshape.271.bias_ref
  20.6 0.2 copy.48
  20.7 0.2 copy.49
  20.9 0.1 copy.50
  21.0 0.1 copy.60
  21.1 0.1 pad_maximum_fusion.2
  21.3 0.2 copy.54
  21.5 0.1 stack.37
  21.6 0.2 pad_maximum_fusion.4
  21.8 0.2 copy.58
  22.0 0.1 stack.42
  22.1 0.4 %pad_maximum_fusion.3 = (bf16[16,4,2,768]{3,1,0,2:T(4,128)(2,1)S(1)}, bf16[16,4,2,768]{3,1,0,2:T(4,128)(2,1)S(1)}) fusion(bf16[16,3,2,768]{3,1,0,2:T(4,128)(2,1)S(1)} %get-tuple-element.7, bf16[16,1,2,768]{3,1,0,2:T(2,128)(2,1)S(1)} %get-tuple-element.5, bf16[16,1,2,768]{3,1,0,2:T(2,128)(2,1)S(1)} %get-tuple-element.6, ...), kind=kLoop, calls=%fused_computation.4 | loop fusion | flops 786432 | bytes 786432 | tf_op jit(solution)/shard_map/jit(_roll_static)/concatenate | solution.py:224
  22.5 0.2 copy.57
  22.7 0.1 stack.41
  22.8 0.2 copy.59
  23.0 0.1 stack.43
  23.1 0.1 tile.8
  23.2 0.3 tile.9
  23.6 0.2 reshape.267
  23.8 0.7 %copy.43 = s32[8,18,16,8]{1,0,3,2:T(8,128)S(1)} copy(s32[8,18,16,8]{2,0,3,1:T(8,128)S(1)} %bitcast.28) | data formatting | bytes 147456 | tf_op jit(solution)/shard_map/transpose | solution.py:239
  24.5 0.2 reshape.268
  24.7 0.1 add_select_fusion
  24.8 0.1 copy.44
  24.9 0.1 reshape.269.where_ref
  24.9 0.1 fusion.1
  25.0 0.1 copy.46
  25.1 0.1 broadcast_in_dim.70
  25.2 0.1 reshape.272.land_ref
  25.4 0.1 pad_maximum_fusion.1.spread
  25.5 0.1 pad_maximum_fusion.taps
  25.6 6.6 %all-to-all-done.inc = bf16[384,8,128]{2,1,0:T(8,128)(2,1)S(1)} async-done(((bf16[384,8,128]{2,1,0:T(8,128)(2,1)}), bf16[384,8,128]{2,1,0:T(8,128)(2,1)S(1)}, u32[]{:S(2)}, u32[]{:S(2)}) %all-to-all-start) | async-done | bytes 786464 | tf_op jit(solution)/shard_map/all_to_all | solution.py:233
  32.2 8.5 %fine.1 = bf16[16,4,288,128]{3,2,1,0:T(8,128)(2,1)} custom-call(s32[200]{0:T(256)S(1)} %reshape.269.where_ref, f32[64]{0:T(128)S(1)} %reshape.271.bias_ref, f32[18,128]{1,0:T(8,128)S(1)} %reshape.272.land_ref, bf16[384,8,128]{2,1,0:T(8,128)(2,1)S(1)} %all-to-all-done.inc, bf16[17,160,128]{2,1,0:T(8,128)(2,1)S(1)} %pad_maximum_fusion.1.spread, ...), custom_call_target="tpu_custom_call" | custom-call | tf_op jit(solution)/shard_map/fine/pallas_call | solution.py:180
  (22 shorter events, 0.3 us)
Async XLA Ops:
  0.0 18.4 %copy-start.2 = (bf16[16,256]{1,0:T(8,128)(2,1)S(1)}, bf16[16,256]{1,0:T(8,128)(2,1)}, u32[]{:S(2)}) copy-start(bf16[16,256]{1,0:T(8,128)(2,1)} %param.9) | copy-start | bytes 24580
  0.0 18.6 %copy-start = (bf16[3,3,64,64]{3,2,1,0:T(8,128)(2,1)S(1)}, bf16[3,3,64,64]{3,2,1,0:T(8,128)(2,1)}, u32[]{:S(2)}) copy-start(bf16[3,3,64,64]{3,2,1,0:T(8,128)(2,1)} %param.10) | copy-start | bytes 221188
  0.0 20.3 %copy-start.3 = (f32[64]{0:T(128)S(1)}, f32[64]{0:T(128)}, u32[]{:S(2)}) copy-start(f32[64]{0:T(128)} %param.11) | copy-start | bytes 772
  3.9 28.3 %all-to-all-start = ((bf16[384,8,128]{2,1,0:T(8,128)(2,1)}), bf16[384,8,128]{2,1,0:T(8,128)(2,1)S(1)}, u32[]{:S(2)}, u32[]{:S(2)}) async-start(bf16[384,8,128]{2,1,0:T(8,128)(2,1)} %pack.1), calls=%async_computation | async-start | bytes 1572864 | tf_op jit(solution)/shard_map/all_to_all | solution.py:233
  19.0 4.5 %copy-start.1 = (s32[128,144]{0,1:T(8,128)S(1)}, s32[128,144]{0,1:T(8,128)}, u32[]{:S(2)}) copy-start(s32[128,144]{0,1:T(8,128)} %param.13) | copy-start | bytes 221188

commit v4 on v3

--- a/solution.py
+++ b/solution.py
@@ -14,13 +14,29 @@
 CB_ROWS = 24
 CB_COLS = 40
 HELD_ROWS = 20
+PART_ROWS = 10
 C_IN = 69
+CHUNK = 4
+STEP = 4
 C = 64
 GRID_COLS = 640
 
 
-def pack_body(ids_ref, coarse_ref, w_ref, out_ref, raw, weights, mixed, sems):
+def pack_body(
+    ids_hbm, coarse_hbm, w_hbm, out_hbm, ids_ref, w_ref, raw, weights, mixed, outgoing, in_sems, out_sems
+):
     n_lat, n_lon = 8, 16
+    ids_copy = pltpu.make_async_copy(ids_hbm.at[0:8, :], ids_ref, in_sems.at[4])
+    ids_copy.start()
+    copies = []
+    for part in range(4):
+        rows = slice(6 * part, 6 * part + 6)
+        copy = pltpu.make_async_copy(coarse_hbm.at[rows], raw.at[rows], in_sems.at[part])
+        copy.start()
+        copies.append(copy)
+    w_copy = pltpu.make_async_copy(w_hbm, w_ref, in_sems.at[5])
+    w_copy.start()
+    ids_copy.wait()
     a = lax.axis_index("lat")
     b = lax.axis_index("lon")
     first = ids_ref[0, 0]
@@ -33,65 +49,82 @@
     lc_first = ((c_first + GRID_COLS) % GRID_COLS) // n_lon
     tile0 = lc_first // 8
     tile1 = (tile0 + 1) % (CB_COLS // 8)
-    copies = []
-    for slot, tile in ((0, tile0), (1, tile1)):
-        copy = pltpu.make_async_copy(
-            coarse_ref.at[pl.ds(low, HELD_ROWS), pl.ds(pl.multiple_of(tile * 8, 8), 8), :],
-            raw.at[slot],
-            sems.at[slot],
-        )
-        copy.start()
-        copies.append(copy)
+    w_copy.wait()
     w = w_ref[...].astype(jnp.float32).T
     weights[...] = jnp.zeros_like(weights)
     for j in range(8):
         weights[j, 10 * j : 10 * j + C_IN, 0:C] = w
         weights[j, 10 * j + C_IN : 10 * j + 2 * C_IN, C : 2 * C] = w
-    for copy in copies:
-        copy.wait()
-    count = 2 * HELD_ROWS * 8
-    for j in range(8):
-        width = min(256, CELLS * C_IN - 128 * j)
-        rows = raw[:, :, :, 128 * j : 128 * j + width].reshape(count, width)
-        part = jnp.dot(
-            rows, weights[j, 0:width, :].astype(jnp.bfloat16), preferred_element_type=jnp.float32
-        )
-        mixed[pl.ds(j, count, stride=8), :] = part
-    starts = []
-    for i in range(n_lat):
-        top = r0 + PR * i - 1
-        r_first = top + (a - top + 512) % n_lat
-        lr = (r_first + 8) // 8 - 1 - low
-        for m in range(MOST):
-            starts.append(jnp.clip(lr + m, 0, HELD_ROWS - 1) * 64)
+    bases = []
     for j in range(n_lon):
         left = c0 + PC * j - 1
         d = (b - left + 16 * CB_COLS) % n_lon
         n = (left + d - c_first) // n_lon
         pos = jnp.minimum(lc_first % 8 + n, 15)
-        base = ((pos // 8) * (HELD_ROWS * 8) + pos % 8) * 8
-        for i in range(n_lat):
-            for m in range(MOST):
-                block = mixed[pl.ds(pl.multiple_of(base + starts[i * MOST + m], 8), 8), :]
-                out_ref[(i * n_lon + j) * MOST + m] = block.astype(jnp.bfloat16)
+        bases.append(((pos // 8) * (PART_ROWS * 8) + pos % 8) * 8)
+    count = 2 * PART_ROWS * 8
+
+    def mix(part):
+        for copy in copies[3 * part : 3 * part + 3]:
+            copy.wait()
+        top = low + PART_ROWS * part
+        for j in range(8):
+            width = min(256, CELLS * C_IN - 128 * j)
+            rows = jnp.concatenate(
+                [
+                    raw[
+                        pl.ds(top, PART_ROWS), pl.ds(pl.multiple_of(tile * 8, 8), 8), 128 * j : 128 * j + width
+                    ].reshape(PART_ROWS * 8, width)
+                    for tile in (tile0, tile1)
+                ],
+                axis=0,
+            )
+            mixed[pl.ds(part * count * 8 + j, count, stride=8), :] = jnp.dot(
+                rows, weights[j, 0:width, :].astype(jnp.bfloat16), preferred_element_type=jnp.float32
+            )
+
+    def send(i):
+        top = r0 + PR * i - 1
+        r_first = top + (a - top + 512) % n_lat
+        lr = (r_first + 8) // 8 - 1 - low
+        for m in range(MOST):
+            row = jnp.clip(lr + m, 0, HELD_ROWS - 1)
+            start = (row + (row // PART_ROWS) * PART_ROWS) * 64
+            for j in range(n_lon):
+                block = mixed[pl.ds(pl.multiple_of(bases[j] + start, 8), 8), :]
+                outgoing[(i * n_lon + j) * MOST + m] = block.astype(jnp.bfloat16)
+        rows = slice(i * n_lon * MOST, (i + 1) * n_lon * MOST)
+        copy = pltpu.make_async_copy(outgoing.at[rows], out_hbm.at[rows], out_sems.at[i])
+        copy.start()
+        return copy
+
+    mix(0)
+    sent = [send(i) for i in range(3)]
+    mix(1)
+    sent += [send(i) for i in range(3, n_lat)]
+    for copy in sent:
+        copy.wait()
 
 
 def pack(block_ids, coarse, w_mix):
     return pl.pallas_call(
         pack_body,
-        out_shape=pltpu.VMEM((128 * MOST, 8, 128), jnp.bfloat16),
-        grid=(1,),
+        out_shape=jax.ShapeDtypeStruct((128 * MOST, 8, 128), jnp.bfloat16),
         in_specs=[
-            pl.BlockSpec((8, 128), lambda g: (0, 0), memory_space=pltpu.SMEM),
             pl.BlockSpec(memory_space=pl.ANY),
-            pl.BlockSpec((C, C_IN), lambda g: (0, 0)),
+            pl.BlockSpec(memory_space=pl.ANY),
+            pl.BlockSpec(memory_space=pl.ANY),
         ],
-        out_specs=pl.BlockSpec(memory_space=pltpu.VMEM),
+        out_specs=pl.BlockSpec(memory_space=pl.ANY),
         scratch_shapes=[
-            pltpu.VMEM((2, HELD_ROWS, 8, CELLS * C_IN), jnp.bfloat16),
+            pltpu.SMEM((8, 128), jnp.int32),
+            pltpu.VMEM((C, C_IN), jnp.bfloat16),
+            pltpu.VMEM((CB_ROWS, CB_COLS, CELLS * C_IN), jnp.bfloat16),
             pltpu.VMEM((8, 256, 2 * C), jnp.float32),
             pltpu.VMEM((2 * HELD_ROWS * 8 * 8, 128), jnp.float32),
-            pltpu.SemaphoreType.DMA((2,)),
+            pltpu.VMEM((128 * MOST, 8, 128), jnp.bfloat16),
+            pltpu.SemaphoreType.DMA((6,)),
+            pltpu.SemaphoreType.DMA((8,)),
         ],
         compiler_params=pltpu.CompilerParams(vmem_limit_bytes=40 << 20),
         name="pack",
@@ -105,7 +138,8 @@
     for o in range(C):
         bias[o] = jnp.full((8, 128), bias_ref[o], jnp.float32)
     lower = lax.broadcasted_iota(jnp.int32, (8, 128), 1) < C
-    for q in range(WR // 2):
+
+    def gather(q):
         for col in range(WC):
             got = []
             for half in range(2):
@@ -115,26 +149,42 @@
             u, v = got
             cells[q, 8 * col : 8 * col + 8, :] = jnp.where(lower, u, pltpu.roll(v, C, 1))
             cells[q, 8 * (WC + col) : 8 * (WC + col) + 8, :] = jnp.where(lower, pltpu.roll(u, C, 1), v)
-    for q in range(WR // 2):
         cells_t[128 * q : 128 * q + 128, :] = cells[q].T.astype(jnp.bfloat16)
 
-    edge = jnp.dot(cells_t[:, 0 : CELLS * WC], spread[16], preferred_element_type=jnp.float32)
-    halo[...] = edge.astype(jnp.bfloat16)
-    lane = lax.broadcasted_iota(jnp.int32, (WR * C, 128), 1)
-    for n in range(4):
-        wide = jnp.concatenate([spread[4 * n + q] for q in range(4)], axis=1)
+    def edges(lo, hi):
+        side = jnp.dot(
+            cells_t[C * lo : C * hi, 0 : CELLS * WC], spread[16], preferred_element_type=jnp.float32
+        )
+        halo[C * lo : C * hi, :] = side.astype(jnp.bfloat16)
+
+    def upsample(lo, hi, first, count):
+        lane = lax.broadcasted_iota(jnp.int32, ((hi - lo) * C, 128), 1)
+        wide = jnp.concatenate([spread[first + q] for q in range(count)], axis=1)
         fine = jnp.dot(
-            cells_t[:, 0 : CELLS * WC], wide, preferred_element_type=jnp.float32
+            cells_t[C * lo : C * hi, 0 : CELLS * WC], wide, preferred_element_type=jnp.float32
         ).astype(jnp.bfloat16)
-        for q in range(4):
-            row = 4 * n + q
+        for q in range(count):
+            row = first + q
             mid = fine[:, 128 * q : 128 * q + 128]
-            side = pltpu.roll(halo[...], 127 - 2 * row, 1)
+            side = pltpu.roll(halo[C * lo : C * hi, :], 127 - 2 * row, 1)
             left = jnp.where(lane == 0, side, pltpu.roll(mid, 1, 1))
             right = jnp.where(lane == 127, side, pltpu.roll(mid, 127, 1))
             for tap, part in enumerate((left, mid, right)):
-                field[tap, :, row] = part.reshape(WR, C, 128)
-    spot = lax.broadcasted_iota(jnp.int32, (16, 8, 128), 1) // 2
+                field[tap, lo:hi, row] = part.reshape(hi - lo, C, 128)
+
+    def pieces(lo, hi):
+        def first_piece():
+            for q in range(lo // 2, hi // 2):
+                gather(q)
+            edges(lo, hi)
+
+        yield first_piece
+        for first in range(0, 16, STEP):
+            low = max(lo, 1) if first + STEP <= 15 else lo
+            high = min(hi, WR - 1) if first > 0 else hi
+            yield lambda low=low, high=high, first=first: upsample(low, high, first, STEP)
+
+    spot = lax.broadcasted_iota(jnp.int32, (8, 128), 0) // 2
 
     def band(step):
         totals = []
@@ -152,26 +202,36 @@
                 jnp.dot(taps[k], jnp.concatenate(columns, axis=1), preferred_element_type=jnp.float32)
             )
         land = land_ref[step : step + 1, :]
-        for u in range(4):
-            halves = []
-            for hb in range(2):
-                t = [total[:, 128 * hb : 128 * hb + 128].reshape(16, 8, 128) for total in totals]
-                got = t[3]
-                for k in range(3):
-                    got = jnp.where(spot == (u + k) % 4, t[k], got)
-                if u > 0:
-                    got = pltpu.roll(got, 8 - 2 * u, 1)
-                halves.append((got + bias[16 * u : 16 * u + 16]) * land)
-            outs[step, :, u] = jnp.concatenate(halves, axis=1).astype(jnp.bfloat16)
+        for v in range(C // 4):
+            for u in range(4):
+                halves = []
+                for hb in range(2):
+                    t = [total[8 * v : 8 * v + 8, 128 * hb : 128 * hb + 128] for total in totals]
+                    got = t[3]
+                    for k in range(3):
+                        got = jnp.where(spot == (u + k) % 4, t[k], got)
+                    if u > 0:
+                        got = pltpu.roll(got, 8 - 2 * u, 0)
+                    halves.append((got + bias[16 * u + v]) * land)
+                outs[4 * v + u, 16 * step : 16 * step + 16, :] = jnp.concatenate(halves, axis=0).astype(jnp.bfloat16)
 
     def store(step):
-        return pltpu.make_async_copy(
-            outs.at[step], out_hbm.at[:, :, step * 16 : step * 16 + 16, :], out_sems.at[step]
-        )
-
-    for step in range(PR):
-        band(step)
-        store(step).start()
+        rows = slice(step * 16, step * 16 + 16)
+        return pltpu.make_async_copy(outs.at[:, rows, :], out_hbm.at[:, rows, :], out_sems.at[step])
+
+    for piece in pieces(0, CHUNK):
+        piece()
+    done = 0
+    for lo in range(CHUNK, WR + CHUNK, CHUNK):
+        ready = min(lo - 2, PR)
+        todo = list(pieces(lo, lo + CHUNK)) if lo < WR else []
+        count = ready - done
+        for n, step in enumerate(range(done, ready)):
+            for piece in todo[n * len(todo) // count : (n + 1) * len(todo) // count]:
+                piece()
+            band(step)
+            store(step).start()
+        done = ready
     for step in range(PR):
         store(step).wait()
 
@@ -179,7 +239,7 @@
 def fine(where, bias_order, land, incoming, spread, taps):
     return pl.pallas_call(
         fine_body,
-        out_shape=jax.ShapeDtypeStruct((C // 4, 4, PR * 16, 128), jnp.bfloat16),
+        out_shape=jax.ShapeDtypeStruct((C, PR * 16, 128), jnp.bfloat16),
         in_specs=[
             pl.BlockSpec(memory_space=pltpu.SMEM),
             pl.BlockSpec(memory_space=pltpu.SMEM),
@@ -195,7 +255,7 @@
             pltpu.VMEM((3, WR, 16, C, 128), jnp.bfloat16),
             pltpu.VMEM((WR * C, 128), jnp.bfloat16),
             pltpu.VMEM((C, 8, 128), jnp.float32),
-            pltpu.VMEM((PR, C // 4, 4, 16, 128), jnp.bfloat16),
+            pltpu.VMEM((C, PR * 16, 128), jnp.bfloat16),
             pltpu.SemaphoreType.DMA((PR,)),
         ],
         compiler_params=pltpu.CompilerParams(vmem_limit_bytes=40 << 20),
@@ -247,8 +307,7 @@
     bias_order = bias.reshape(C // 4, 4).T.reshape(C)
     near = (land, incoming, spread_of(interp), taps_of(kernel))
     near = tuple(pltpu.with_memory_space_constraint(v, pltpu.VMEM) for v in near)
-    out = fine(where, bias_order, *near)
-    return out.reshape(C, PR * 16, 128)
+    return fine(where, bias_order, *near)
 
 
 def solution(mesh):

time: 41 us -> 40.5 us (0.988)
  Pallas kernels: 12.4 us -> 11.9 us
    pallas_call x2, Pallas kernels: 12.4 us -> 11.9 us  [the longest x1 8.36 us: fine(): pl.pallas_call(fine_body, out_shape=jax.ShapeDtypeStruct((C, PR * 16, 128...]
where the time goes in v4:
time: 40.5 us; the launch traced here: 40.2 us
  Pallas kernels  11.9 us (29%)
  starting transfers between devices  11.5 us (28%)
  local copies, waits for them, and re-layouts  6.76 us (17%)
  waiting for transfers between devices  6.55 us (16%)
  between operations  2.22 us (5%)
  other arithmetic  1.25 us (3%)
    all_to_all x1, starting transfers between devices, per_device(): lax.all_to_all(outgoing, ('lat', 'lon'), split_axis=0, concat_axis=0, til...  11.5 us
    pallas_call x1, Pallas kernels, fine(): pl.pallas_call(fine_body, out_shape=jax.ShapeDtypeStruct((C, PR * 16, 128...  8.36 us
    all_to_all x1, waiting for transfers between devices, per_device(): lax.all_to_all(outgoing, ('lat', 'lon'), split_axis=0, concat_axis=0, til...  6.55 us
    pallas_call x1, Pallas kernels, pack(): pl.pallas_call(pack_body, out_shape=jax.ShapeDtypeStruct((128 * MOST, 8,...  3.54 us
    slice x1, local copies, waits for them, and re-layouts, per_device(): first = block_ids[0, 0]  1.2 us
    another operation x6, local copies, waits for them, and re-layouts, taps_of(): jnp.stack([jnp.pad(by, ((0, 0), (0, 0), (r, 1 - r), (0, 0))) for r in ran...  0.82 us
  transfers between devices with their start and end apart: 1, of which 1 were waited for; matrix products, arithmetic and copies ran while one was open for 20% of the time, Pallas kernels for 0%

profile of v4, /device:TPU:1, one launch (start us, length us, event | category | flops | bytes accessed | tf_op | source)
XLA Modules:
  0.0 40.2 jit_solution(3173303332364105118)
XLA Ops:
  0.0 3.5 %pack.1 = bf16[384,8,128]{2,1,0:T(8,128)(2,1)} custom-call(s32[144,128]{1,0:T(8,128)} %bitcast.34, bf16[24,40,1104]{2,1,0:T(8,128)(2,1)} %bitcast.28, bf16[64,69]{1,0:T(8,128)(2,1)} %bitcast.37), custom_call_target="tpu_custom_call" | custom-call | tf_op jit(solution)/shard_map/pack/pallas_call | solution.py:110
  3.6 11.5 %all-to-all-start = ((bf16[384,8,128]{2,1,0:T(8,128)(2,1)}), bf16[384,8,128]{2,1,0:T(8,128)(2,1)S(1)}, u32[]{:S(2)}, u32[]{:S(2)}) async-start(bf16[384,8,128]{2,1,0:T(8,128)(2,1)} %pack.1), calls=%async_computation | async-start | bytes 1572864 | tf_op jit(solution)/shard_map/all_to_all | solution.py:293
  15.1 1.2 %slice.36 = s32[1,1]{0,1:T(1,128)} slice(s32[128,144]{0,1:T(8,128)} %param.12), slice={[0:1], [0:1]} | slice | bytes 8 | tf_op jit(solution)/shard_map/slice | solution.py:294
  18.0 0.1 reshape.271
  18.2 0.1 fusion.10
  18.3 0.1 copy.61
  18.4 0.2 fusion.9
  18.7 0.1 stack.39
  18.8 0.1 stack.35
  19.0 0.1 stack.38
  19.1 0.1 stack.34
  19.4 0.1 fusion.8
  19.5 0.1 fusion.6
  19.7 0.1 fusion.7
  19.9 0.1 reshape.267
  20.0 0.1 copy.45
  20.1 0.1 reshape.268.bias_ref
  20.2 0.2 copy.48
  20.4 0.2 copy.49
  20.6 0.1 copy.50
  20.7 0.1 copy.60
  20.8 0.1 pad_maximum_fusion.2
  20.9 0.2 copy.54
  21.1 0.1 stack.37
  21.2 0.2 pad_maximum_fusion.4
  21.4 0.2 copy.58
  21.6 0.1 stack.42
  21.7 0.4 %pad_maximum_fusion.3 = (bf16[16,4,2,768]{3,1,0,2:T(4,128)(2,1)S(1)}, bf16[16,4,2,768]{3,1,0,2:T(4,128)(2,1)S(1)}) fusion(bf16[16,3,2,768]{3,1,0,2:T(4,128)(2,1)S(1)} %get-tuple-element.7, bf16[16,1,2,768]{3,1,0,2:T(2,128)(2,1)S(1)} %get-tuple-element.5, bf16[16,1,2,768]{3,1,0,2:T(2,128)(2,1)S(1)} %get-tuple-element.6, ...), kind=kLoop, calls=%fused_computation.4 | loop fusion | flops 786432 | bytes 786432 | tf_op jit(solution)/shard_map/jit(_roll_static)/concatenate | solution.py:284
  22.1 0.2 copy.57
  22.3 0.1 stack.41
  22.4 0.2 copy.59
  22.6 0.1 stack.43
  22.7 0.1 tile.8
  22.8 0.3 tile.9
  23.2 0.2 reshape.264
  23.4 0.7 %copy.43 = s32[8,18,16,8]{1,0,3,2:T(8,128)S(1)} copy(s32[8,18,16,8]{2,0,3,1:T(8,128)S(1)} %bitcast.27) | data formatting | bytes 147456 | tf_op jit(solution)/shard_map/transpose | solution.py:299
  24.1 0.2 reshape.265
  24.3 0.1 add_select_fusion
  24.4 0.1 copy.44
  24.5 0.1 reshape.266.where_ref
  24.6 0.1 fusion.1
  24.7 0.1 copy.46
  24.8 0.1 broadcast_in_dim.70
  24.8 0.1 reshape.269.land_ref
  25.1 0.1 pad_maximum_fusion.1.spread
  25.1 0.1 pad_maximum_fusion.taps
  25.3 6.6 %all-to-all-done.inc = bf16[384,8,128]{2,1,0:T(8,128)(2,1)S(1)} async-done(((bf16[384,8,128]{2,1,0:T(8,128)(2,1)}), bf16[384,8,128]{2,1,0:T(8,128)(2,1)S(1)}, u32[]{:S(2)}, u32[]{:S(2)}) %all-to-all-start) | async-done | bytes 786464 | tf_op jit(solution)/shard_map/all_to_all | solution.py:293
  31.8 8.4 %fine.1 = bf16[64,288,128]{2,1,0:T(8,128)(2,1)} custom-call(s32[200]{0:T(256)S(1)} %reshape.266.where_ref, f32[64]{0:T(128)S(1)} %reshape.268.bias_ref, f32[18,128]{1,0:T(8,128)S(1)} %reshape.269.land_ref, bf16[384,8,128]{2,1,0:T(8,128)(2,1)S(1)} %all-to-all-done.inc, bf16[17,160,128]{2,1,0:T(8,128)(2,1)S(1)} %pad_maximum_fusion.1.spread, ...), custom_call_target="tpu_custom_call" | custom-call | tf_op jit(solution)/shard_map/fine/pallas_call | solution.py:240
  (22 shorter events, 0.3 us)
Async XLA Ops:
  0.0 18.0 %copy-start.2 = (bf16[16,256]{1,0:T(8,128)(2,1)S(1)}, bf16[16,256]{1,0:T(8,128)(2,1)}, u32[]{:S(2)}) copy-start(bf16[16,256]{1,0:T(8,128)(2,1)} %param.9) | copy-start | bytes 24580
  0.0 18.3 %copy-start = (bf16[3,3,64,64]{3,2,1,0:T(8,128)(2,1)S(1)}, bf16[3,3,64,64]{3,2,1,0:T(8,128)(2,1)}, u32[]{:S(2)}) copy-start(bf16[3,3,64,64]{3,2,1,0:T(8,128)(2,1)} %param.10) | copy-start | bytes 221188
  0.0 19.9 %copy-start.3 = (f32[64]{0:T(128)S(1)}, f32[64]{0:T(128)}, u32[]{:S(2)}) copy-start(f32[64]{0:T(128)} %param.11) | copy-start | bytes 772
  3.6 28.3 %all-to-all-start = ((bf16[384,8,128]{2,1,0:T(8,128)(2,1)}), bf16[384,8,128]{2,1,0:T(8,128)(2,1)S(1)}, u32[]{:S(2)}, u32[]{:S(2)}) async-start(bf16[384,8,128]{2,1,0:T(8,128)(2,1)} %pack.1), calls=%async_computation | async-start | bytes 1572864 | tf_op jit(solution)/shard_map/all_to_all | solution.py:293
  18.7 4.5 %copy-start.1 = (s32[128,144]{0,1:T(8,128)S(1)}, s32[128,144]{0,1:T(8,128)}, u32[]{:S(2)}) copy-start(s32[128,144]{0,1:T(8,128)} %param.13) | copy-start | bytes 221188

commit v5 on v4

--- a/solution.py
+++ b/solution.py
@@ -14,7 +14,7 @@
 CB_ROWS = 24
 CB_COLS = 40
 HELD_ROWS = 20
-PART_ROWS = 10
+PART_ROWS = 20
 C_IN = 69
 CHUNK = 4
 STEP = 4
@@ -65,7 +65,7 @@
     count = 2 * PART_ROWS * 8
 
     def mix(part):
-        for copy in copies[3 * part : 3 * part + 3]:
+        for copy in copies:
             copy.wait()
         top = low + PART_ROWS * part
         for j in range(8):
@@ -100,7 +100,6 @@
 
     mix(0)
     sent = [send(i) for i in range(3)]
-    mix(1)
     sent += [send(i) for i in range(3, n_lat)]
     for copy in sent:
         copy.wait()

time: 40.5 us -> 40.4 us (level)
  no operation moved by 1% of the time
where the time goes in v5:
time: 40.4 us; the launch traced here: 40.1 us
  Pallas kernels  11.8 us (29%)
  starting transfers between devices  11.5 us (28%)
  local copies, waits for them, and re-layouts  6.76 us (17%)
  waiting for transfers between devices  6.55 us (16%)
  between operations  2.22 us (5%)
  other arithmetic  1.25 us (3%)
    all_to_all x1, starting transfers between devices, per_device(): lax.all_to_all(outgoing, ('lat', 'lon'), split_axis=0, concat_axis=0, til...  11.5 us
    pallas_call x1, Pallas kernels, fine(): pl.pallas_call(fine_body, out_shape=jax.ShapeDtypeStruct((C, PR * 16, 128...  8.35 us
    all_to_all x1, waiting for transfers between devices, per_device(): lax.all_to_all(outgoing, ('lat', 'lon'), split_axis=0, concat_axis=0, til...  6.55 us
    pallas_call x1, Pallas kernels, pack(): pl.pallas_call(pack_body, out_shape=jax.ShapeDtypeStruct((128 * MOST, 8,...  3.46 us
    slice x1, local copies, waits for them, and re-layouts, per_device(): first = block_ids[0, 0]  1.2 us
    another operation x6, local copies, waits for them, and re-layouts, taps_of(): jnp.stack([jnp.pad(by, ((0, 0), (0, 0), (r, 1 - r), (0, 0))) for r in ran...  0.82 us
  transfers between devices with their start and end apart: 1, of which 1 were waited for; matrix products, arithmetic and copies ran while one was open for 20% of the time, Pallas kernels for 0%

profile of v5, /device:TPU:1, one launch (start us, length us, event | category | flops | bytes accessed | tf_op | source)
XLA Modules:
  0.0 40.1 jit_solution(12759812146872762145)
XLA Ops:
  0.0 3.5 %pack.1 = bf16[384,8,128]{2,1,0:T(8,128)(2,1)} custom-call(s32[144,128]{1,0:T(8,128)} %bitcast.34, bf16[24,40,1104]{2,1,0:T(8,128)(2,1)} %bitcast.28, bf16[64,69]{1,0:T(8,128)(2,1)} %bitcast.37), custom_call_target="tpu_custom_call" | custom-call | tf_op jit(solution)/shard_map/pack/pallas_call | solution.py:109
  3.5 11.5 %all-to-all-start = ((bf16[384,8,128]{2,1,0:T(8,128)(2,1)}), bf16[384,8,128]{2,1,0:T(8,128)(2,1)S(1)}, u32[]{:S(2)}, u32[]{:S(2)}) async-start(bf16[384,8,128]{2,1,0:T(8,128)(2,1)} %pack.1), calls=%async_computation | async-start | bytes 1572864 | tf_op jit(solution)/shard_map/all_to_all | solution.py:292
  15.0 1.2 %slice.36 = s32[1,1]{0,1:T(1,128)} slice(s32[128,144]{0,1:T(8,128)} %param.12), slice={[0:1], [0:1]} | slice | bytes 8 | tf_op jit(solution)/shard_map/slice | solution.py:293
  18.0 0.1 reshape.271
  18.1 0.1 fusion.10
  18.2 0.1 copy.61
  18.3 0.2 fusion.9
  18.6 0.1 stack.39
  18.7 0.1 stack.35
  18.9 0.1 stack.38
  19.0 0.1 stack.34
  19.3 0.1 fusion.8
  19.4 0.1 fusion.6
  19.6 0.1 fusion.7
  19.9 0.1 reshape.267
  19.9 0.1 copy.45
  20.0 0.1 reshape.268.bias_ref
  20.1 0.2 copy.48
  20.3 0.2 copy.49
  20.5 0.1 copy.50
  20.6 0.1 copy.60
  20.7 0.1 pad_maximum_fusion.2
  20.8 0.2 copy.54
  21.0 0.1 stack.37
  21.1 0.2 pad_maximum_fusion.4
  21.3 0.2 copy.58
  21.6 0.1 stack.42
  21.6 0.4 %pad_maximum_fusion.3 = (bf16[16,4,2,768]{3,1,0,2:T(4,128)(2,1)S(1)}, bf16[16,4,2,768]{3,1,0,2:T(4,128)(2,1)S(1)}) fusion(bf16[16,3,2,768]{3,1,0,2:T(4,128)(2,1)S(1)} %get-tuple-element.7, bf16[16,1,2,768]{3,1,0,2:T(2,128)(2,1)S(1)} %get-tuple-element.5, bf16[16,1,2,768]{3,1,0,2:T(2,128)(2,1)S(1)} %get-tuple-element.6, ...), kind=kLoop, calls=%fused_computation.4 | loop fusion | flops 786432 | bytes 786432 | tf_op jit(solution)/shard_map/jit(_roll_static)/concatenate | solution.py:283
  22.1 0.2 copy.57
  22.3 0.1 stack.41
  22.4 0.2 copy.59
  22.6 0.1 stack.43
  22.6 0.1 tile.8
  22.8 0.3 tile.9
  23.1 0.2 reshape.264
  23.3 0.7 %copy.43 = s32[8,18,16,8]{1,0,3,2:T(8,128)S(1)} copy(s32[8,18,16,8]{2,0,3,1:T(8,128)S(1)} %bitcast.27) | data formatting | bytes 147456 | tf_op jit(solution)/shard_map/transpose | solution.py:298
  24.0 0.2 reshape.265
  24.2 0.1 add_select_fusion
  24.3 0.1 copy.44
  24.4 0.1 reshape.266.where_ref
  24.5 0.1 fusion.1
  24.6 0.1 copy.46
  24.7 0.1 broadcast_in_dim.70
  24.8 0.1 reshape.269.land_ref
  25.0 0.1 pad_maximum_fusion.1.spread
  25.1 0.1 pad_maximum_fusion.taps
  25.2 6.6 %all-to-all-done.inc = bf16[384,8,128]{2,1,0:T(8,128)(2,1)S(1)} async-done(((bf16[384,8,128]{2,1,0:T(8,128)(2,1)}), bf16[384,8,128]{2,1,0:T(8,128)(2,1)S(1)}, u32[]{:S(2)}, u32[]{:S(2)}) %all-to-all-start) | async-done | bytes 786464 | tf_op jit(solution)/shard_map/all_to_all | solution.py:292
  31.7 8.4 %fine.1 = bf16[64,288,128]{2,1,0:T(8,128)(2,1)} custom-call(s32[200]{0:T(256)S(1)} %reshape.266.where_ref, f32[64]{0:T(128)S(1)} %reshape.268.bias_ref, f32[18,128]{1,0:T(8,128)S(1)} %reshape.269.land_ref, bf16[384,8,128]{2,1,0:T(8,128)(2,1)S(1)} %all-to-all-done.inc, bf16[17,160,128]{2,1,0:T(8,128)(2,1)S(1)} %pad_maximum_fusion.1.spread, ...), custom_call_target="tpu_custom_call" | custom-call | tf_op jit(solution)/shard_map/fine/pallas_call | solution.py:239
  (22 shorter events, 0.3 us)
Async XLA Ops:
  0.0 18.0 %copy-start.2 = (bf16[16,256]{1,0:T(8,128)(2,1)S(1)}, bf16[16,256]{1,0:T(8,128)(2,1)}, u32[]{:S(2)}) copy-start(bf16[16,256]{1,0:T(8,128)(2,1)} %param.9) | copy-start | bytes 24580
  0.0 18.2 %copy-start = (bf16[3,3,64,64]{3,2,1,0:T(8,128)(2,1)S(1)}, bf16[3,3,64,64]{3,2,1,0:T(8,128)(2,1)}, u32[]{:S(2)}) copy-start(bf16[3,3,64,64]{3,2,1,0:T(8,128)(2,1)} %param.10) | copy-start | bytes 221188
  0.0 19.9 %copy-start.3 = (f32[64]{0:T(128)S(1)}, f32[64]{0:T(128)}, u32[]{:S(2)}) copy-start(f32[64]{0:T(128)} %param.11) | copy-start | bytes 772
  3.5 28.3 %all-to-all-start = ((bf16[384,8,128]{2,1,0:T(8,128)(2,1)}), bf16[384,8,128]{2,1,0:T(8,128)(2,1)S(1)}, u32[]{:S(2)}, u32[]{:S(2)}) async-start(bf16[384,8,128]{2,1,0:T(8,128)(2,1)} %pack.1), calls=%async_computation | async-start | bytes 1572864 | tf_op jit(solution)/shard_map/all_to_all | solution.py:292
  18.6 4.5 %copy-start.1 = (s32[128,144]{0,1:T(8,128)S(1)}, s32[128,144]{0,1:T(8,128)}, u32[]{:S(2)}) copy-start(s32[128,144]{0,1:T(8,128)} %param.13) | copy-start | bytes 221188
